TPU v7x, 256 devices: a whole 4x4x8 slice. The times are simulated.
256 devices in a mesh: blk: 4 (over y), py: 8 (over z), pz: 8 (over x, core).
Axes of the slice: x: 4, y: 4, z: 8, core: 2. Of those that a mesh axis runs over, the one named last changes fastest.
Arguments:
- source: float32 [256, 1024, 128], P(('py', 'pz'), 'blk'), may hold values from -6 to 6
- conduct: float32 [3], replicated, may hold values from 0.3 to 3
- neighbours: int32 [4, 2], replicated, may hold values from -1 to 3, as said below
- orient: int32 [4], replicated, may hold values 0 or 1
Outputs:
- solution: float32 [256, 1024, 128], P(('py', 'pz'), 'blk')
- norms: float32 [3], replicated
Inputs may be any that keep to these rules, and one draw needn't show every extreme that they name: `neighbours`: the blocks form one chain: row b holds the left and the right neighbour of block b, -1 marks the two ends, and a block is the left neighbour of its right neighbour.
All inputs are finite; a program needn't handle non-finite values.
Results may differ from a plain program's by a relative error of at most 0.00011.
Values sent between devices are 32-bit elements; how exact they have to be, the bound alone decides.
A program may use at most 64 MiB of HBM per device.

v0:
```python
import functools

import jax
import jax.numpy as jnp
from jax import lax
from jax.sharding import Mesh
from jax.sharding import PartitionSpec as P

NY = 256
NZ = 128
BX = 256
OV = 64
ITERS = 3
EXT = 384
PZ = ("pz_0", "pz_1")
PY_PZ = ("py", "pz_0", "pz_1")
BLK_PY_PZ = ("blk", "py", "pz_0", "pz_1")


HIGHEST = lax.Precision.HIGHEST


def cut_along(x, dim, devices):
    shape = x.shape
    blocks = x.reshape(*shape[:dim], devices, shape[dim] // devices, *shape[dim + 1 :])
    return jnp.moveaxis(blocks, dim, 0)


def joined_along(blocks, dim):
    shape = list(blocks.shape[1:])
    shape[dim] *= blocks.shape[0]
    return jnp.moveaxis(blocks, 0, dim).reshape(shape)


def one_exchange(x, axis, axes, splits, concats):
    sizes = [lax.axis_size(a) for a in axes]
    blocks = cut_along(x, splits[0], sizes[0])
    blocks = jnp.moveaxis(cut_along(blocks, splits[1] + 1, sizes[1]), 0, 1)
    inside = blocks.shape[2:]
    blocks = blocks.reshape(-1, *inside)
    blocks = lax.all_to_all(blocks, axis, split_axis=0, concat_axis=0, tiled=True)
    blocks = joined_along(blocks.reshape(*sizes, *inside), concats[0] + 1)
    return joined_along(blocks, concats[1])


def extended_2(cells, sides, width):
    for axis, dim in sides:
        count = lax.axis_size(axis)
        ends = count - 1
        head = lax.slice_in_dim(cells, 0, width, axis=dim)
        tail = lax.slice_in_dim(cells, cells.shape[dim] - width, cells.shape[dim], axis=dim)
        cells = jnp.concatenate(
            [
                lax.ppermute(tail, axis, [(i, (i + 1) % count) for i in range(ends)]),
                cells,
                lax.ppermute(head, axis, [((i + 1) % count, i) for i in range(ends)]),
            ],
            axis=dim,
        )
    return cells


def one_axis_at_a_time(x, axes):
    return functools.reduce(lax.psum, axes, x)


def sine_basis(row_index, col_index, length):
    product = (row_index[:, None] + 1) * (col_index[None, :] + 1) % (2 * (length + 1))
    angles = jnp.pi * product.astype(jnp.float32) / (length + 1)
    return jnp.sqrt(2.0 / (length + 1)) * jnp.sin(angles)


def spectrum(index, length):
    angles = jnp.pi * (index.astype(jnp.float32) + 1.0) / (2.0 * (length + 1))
    return 4.0 * jnp.sin(angles) ** 2


def pick_block(pool, block_ids, wanted):
    match = (block_ids == wanted)[:, None, None, None]
    return jnp.sum(jnp.where(match, pool, 0.0), axis=0)


def outgoing(low_end, high_end, neighbours, own_block):
    left_of = (neighbours[:, 0] == own_block)[:, None, None, None]
    right_of = (neighbours[:, 1] == own_block)[:, None, None, None]
    return jnp.where(left_of, high_end[None], jnp.where(right_of, low_end[None], 0.0))


def shards(source, conduct, neighbours, orient):
    row_count = source.shape[0]
    blocks = neighbours.shape[0]
    own_block = lax.axis_index("blk")
    block_ids = jnp.arange(blocks, dtype=jnp.int32)
    chosen = block_ids == own_block
    left_id = jnp.sum(jnp.where(chosen, neighbours[:, 0], 0))
    right_id = jnp.sum(jnp.where(chosen, neighbours[:, 1], 0))
    flipped = jnp.sum(jnp.where(chosen, orient, 0)) == 1
    has_left = (left_id >= 0).astype(jnp.float32)
    has_right = (right_id >= 0).astype(jnp.float32)
    planes_src = jnp.where(flipped, source[:, ::-1, :], source)
    size_py = lax.axis_size("py")
    size_pz = lax.axis_size(PZ)
    group_size = size_py * size_pz
    group_width = EXT // group_size
    column_group = lax.axis_index("py") * size_pz + lax.axis_index(PZ)
    plane_ids = jnp.arange(EXT, dtype=jnp.int32)
    row_ids = jnp.arange(NY, dtype=jnp.int32)
    depth_ids = jnp.arange(NZ, dtype=jnp.int32)
    plane_basis = sine_basis(plane_ids, plane_ids, EXT)
    row_basis = sine_basis(row_ids, row_ids, NY)
    depth_basis = sine_basis(depth_ids, depth_ids, NZ)
    row_block = row_ids // row_count
    true_rows = (
        row_block % size_py * size_pz + row_block // size_py
    ) * row_count + row_ids % row_count
    row_forward = sine_basis(true_rows, row_ids, NY)
    place_block = plane_ids // group_width
    true_modes = (
        place_block % size_py * size_pz + place_block // size_py
    ) * group_width + plane_ids % group_width
    plane_back = sine_basis(plane_ids, true_modes, EXT)
    held_modes = column_group * group_width + jnp.arange(group_width, dtype=jnp.int32)
    spectra = (
        conduct[0] * spectrum(held_modes, EXT)[None, :, None]
        + conduct[1] * spectrum(row_ids, NY)[:, None, None]
        + conduct[2] * spectrum(depth_ids, NZ)[None, None, :]
    )
    received = lax.all_to_all(
        outgoing(planes_src[:, :OV, :], planes_src[:, BX - OV :, :], neighbours, own_block),
        "blk",
        split_axis=0,
        concat_axis=0,
        tiled=True,
    )
    from_left = pick_block(received, block_ids, left_id)
    from_right = pick_block(received, block_ids, right_id)
    source_ext = jnp.concatenate([from_left, planes_src, from_right], axis=1)
    plane_mask = jnp.where(
        plane_ids < OV, has_left, jnp.where(plane_ids >= OV + BX, has_right, 1.0)
    )[None, :, None]
    cell_count = float(blocks * BX * NY * NZ)
    iterate = jnp.zeros_like(planes_src)
    square_sums = []
    for iteration in range(ITERS):
        if iteration == 0:
            residual = source_ext * plane_mask
        else:
            iterate_received = lax.all_to_all(
                outgoing(
                    iterate[:, : OV + 1, :], iterate[:, BX - OV - 1 :, :], neighbours, own_block
                ),
                "blk",
                split_axis=0,
                concat_axis=0,
                tiled=True,
            )
            iterate_left = pick_block(iterate_received, block_ids, left_id)
            iterate_right = pick_block(iterate_received, block_ids, right_id)
            extended = jnp.concatenate([iterate_left, iterate, iterate_right], axis=1)
            centre = extended[:, 1:-1, :]
            rows_pad = extended_2(centre, ((PY_PZ, 0),), 1)
            depth_pad = jnp.pad(centre, ((0, 0), (0, 0), (1, 1)))
            applied = (
                conduct[0] * (2.0 * centre - extended[:, :-2, :] - extended[:, 2:, :])
                + conduct[1] * (2.0 * centre - rows_pad[:-2] - rows_pad[2:])
                + conduct[2] * (2.0 * centre - depth_pad[:, :, :-2] - depth_pad[:, :, 2:])
            )
            residual = (source_ext - applied) * plane_mask
        own_squares = jnp.sum(residual[:, OV : OV + BX, :] ** 2)
        square_sums.append(one_axis_at_a_time(own_squares, BLK_PY_PZ))
        modes = jnp.einsum("yxz,xk->ykz", residual, plane_basis, precision=HIGHEST)
        columns = one_exchange(modes, PY_PZ, ("py", PZ), (1, 1), (0, 0))
        columns = jnp.einsum("lxz,lm->mxz", columns, row_forward, precision=HIGHEST)
        columns = jnp.einsum("yxz,zk->yxk", columns, depth_basis, precision=HIGHEST)
        columns = columns / spectra
        columns = jnp.einsum("yxz,zk->yxk", columns, depth_basis, precision=HIGHEST)
        columns = jnp.einsum("mxz,ym->yxz", columns, row_basis, precision=HIGHEST)
        returned = one_exchange(columns, PY_PZ, ("py", PZ), (0, 0), (1, 1))
        iterate = (
            iterate
            + jnp.einsum("ypz,xp->yxz", returned, plane_back, precision=HIGHEST)[:, OV : OV + BX, :]
        )
    norms = jnp.sqrt(jnp.stack(square_sums) / cell_count)
    solution = jnp.where(flipped, iterate[:, ::-1, :], iterate)
    return (solution, norms)


def solution(mesh):
    torus = Mesh(
        mesh.devices.reshape(mesh.shape["blk"], mesh.shape["py"], 4, 2),
        ("blk", "py", "pz_0", "pz_1"),
    )
    placed = (P(PY_PZ, "blk", None), P(), P(), P())
    return jax.shard_map(
        shards, mesh=torus, in_specs=placed, out_specs=(P(PY_PZ, "blk", None), P()), check_vma=False
    )
```

profile of v0, /device:TPU:1, one launch (start us, length us, event | category | flops | bytes accessed | tf_op | source)
XLA Modules:
  0.0 339.9 jit_solution(7045087397192263017)
XLA Ops:
  0.6 1.3 select_reduce_fusion.6
  2.8 3.4 %rev.6 = f32[4,256,128]{2,1,0:T(8,128)S(1)} reverse(f32[4,256,128]{2,1,0:T(8,128)} %param.4), dimensions={1} | reverse | bytes 1048576 | tf_op jit(solution)/shard_map/rev | solution.py:100
  7.9 5.0 %all-to-all-start = ((f32[4,4,64,128]{3,2,1,0:T(8,128)}), f32[4,4,64,128]{3,2,1,0:T(8,128)S(1)}, u32[]{:S(2)}, u32[]{:S(2)}) async-start(f32[4,4,64,128]{3,2,1,0:T(8,128)} %select_select_fusion.2), calls=%async_computation | async-start | bytes 1048576 | tf_op jit(solution)/shard_map/all_to_all | solution.py:128
  14.9 1.3 iota_compare_fusion.2
  16.2 4.3 %all-to-all-done = f32[4,4,64,128]{3,2,1,0:T(8,128)S(1)} async-done(((f32[4,4,64,128]{3,2,1,0:T(8,128)}), f32[4,4,64,128]{3,2,1,0:T(8,128)S(1)}, u32[]{:S(2)}, u32[]{:S(2)}) %all-to-all-start) | async-done | bytes 524320 | tf_op jit(solution)/shard_map/all_to_all | solution.py:128
  20.8 3.7 %fusion.47 = f32[384,4,128]{2,0,1:T(8,128)S(1)} fusion(f32[4,384,128]{2,1,0:T(8,128)S(1)} %broadcast_multiply_fusion, s32[384]{0:T(512)S(1)} %get-tuple-element.42), kind=kOutput, calls=%fused_computation.74 | convolution fusion | flops 907444224 | bytes 1574400 | tf_op jit(solution)/shard_map/yxz,xk->ykz/dot_general | solution.py:171
  25.1 1.4 copy.126
  26.5 14.7 %all-to-all-start.1 = ((f32[64,4,6,128]{3,1,2,0:T(4,128)}), f32[64,4,6,128]{3,1,2,0:T(4,128)S(1)}, u32[]{:S(2)}, u32[]{:S(2)}) async-start(f32[64,4,6,128]{3,1,2,0:T(4,128)} %copy.126), calls=%async_computation.1 | async-start | bytes 1572864 | tf_op jit(solution)/shard_map/all_to_all | solution.py:41
  44.0 20.0 %all-to-all-done.1 = f32[64,4,6,128]{3,1,2,0:T(4,128)S(1)} async-done(((f32[64,4,6,128]{3,1,2,0:T(4,128)}), f32[64,4,6,128]{3,1,2,0:T(4,128)S(1)}, u32[]{:S(2)}, u32[]{:S(2)}) %all-to-all-start.1) | async-done | bytes 786464 | tf_op jit(solution)/shard_map/all_to_all | solution.py:41
  64.7 1.9 fusion.114
  66.7 1.1 add_divide_fusion.2
  67.7 1.1 fusion.166
  68.8 1.9 fusion.107
  70.9 28.9 %all_to_all.45 = f32[64,4,6,128]{3,1,2,0:T(4,128)S(1)} all-to-all(f32[64,4,6,128]{3,1,2,0:T(4,128)S(1)} %copy.130), channel_id=1, replica_groups=mesh['blk'=4,'py'=8,'pz_0'=4,'pz_1'=2] {'py','pz_0','pz_1'}, dimensions={0} | all-to-all | bytes 1572864 | tf_op jit(solution)/shard_map/all_to_all | solution.py:41
  100.2 3.7 %convolution_bitcast_fusion.2 = f32[4,384,128]{2,1,0:T(8,128)S(1)} fusion(f32[4,384,128]{2,1,0:T(8,128)S(1)} %bitcast.175, s32[384]{0:T(512)S(1)} %get-tuple-element.41, s32[384]{0:T(512)S(1)} %get-tuple-element.42), kind=kOutput, calls=%fused_computation.9 | convolution fusion | flops 907444224 | bytes 1575936 | tf_op jit(solution)/shard_map/ypz,xp->yxz/dot_general | solution.py:181
  105.0 3.5 %all-to-all-start.3 = ((f32[4,4,65,128]{3,1,2,0:T(4,128)}), f32[4,4,65,128]{3,1,2,0:T(4,128)S(1)}, u32[]{:S(2)}, u32[]{:S(2)}) async-start(f32[4,4,65,128]{3,1,2,0:T(4,128)} %select_select_fusion.1), calls=%async_computation.3 | async-start | bytes 1064960 | tf_op jit(solution)/shard_map/all_to_all | solution.py:148
  108.5 8.9 %all-to-all-done.3 = f32[4,4,65,128]{3,1,2,0:T(4,128)S(1)} async-done(((f32[4,4,65,128]{3,1,2,0:T(4,128)}), f32[4,4,65,128]{3,1,2,0:T(4,128)S(1)}, u32[]{:S(2)}, u32[]{:S(2)}) %all-to-all-start.3) | async-done | bytes 532512 | tf_op jit(solution)/shard_map/all_to_all | solution.py:148
  117.9 4.2 %collective-permute-start = (f32[1,384,128]{2,1,0:T(8,128)S(1)}, f32[1,384,128]{2,1,0:T(8,128)S(1)}, u32[]{:S(2)}, u32[]{:S(2)}) collective-permute-start(f32[1,384,128]{2,1,0:T(8,128)S(1)} %get-tuple-element.24), channel_id=1, source_target_pairs={{0,1},{1,2},{2,3},{3,4},{4,5},{5,6},{6,7},{7,8},{8,9},{9,10},{10,1... | collective-permute-start | bytes 589832 | tf_op jit(solution)/shard_map/ppermute | solution.py:54
  122.1 1.9 collective-permute-start.1
  124.7 4.4 %collective-permute-done.1 = f32[1,384,128]{2,1,0:T(8,128)S(1)} collective-permute-done((f32[1,384,128]{2,1,0:T(8,128)S(1)}, f32[1,384,128]{2,1,0:T(8,128)S(1)}, u32[]{:S(2)}, u32[]{:S(2)}) %collective-permute-start.1) | collective-permute-done | bytes 196640 | tf_op jit(solution)/shard_map/ppermute | solution.py:56
  129.1 2.5 fusion.5
  131.6 3.7 %fusion.45 = f32[384,4,128]{2,0,1:T(8,128)S(1)} fusion(f32[4,384,128]{2,1,0:T(8,128)S(1)} %fusion.5, s32[384]{0:T(512)S(1)} %copy-done.22), kind=kOutput, calls=%fused_computation.73 | convolution fusion | flops 907444224 | bytes 1574400 | tf_op jit(solution)/shard_map/yxz,xk->ykz/dot_general | solution.py:171
  136.3 32.4 %all_to_all.46 = f32[64,4,6,128]{3,1,2,0:T(4,128)S(1)} all-to-all(f32[64,4,6,128]{3,1,2,0:T(4,128)S(1)} %copy.141), channel_id=1, replica_groups=mesh['blk'=4,'py'=8,'pz_0'=4,'pz_1'=2] {'py','pz_0','pz_1'}, dimensions={0} | all-to-all | bytes 1572864 | tf_op jit(solution)/shard_map/all_to_all | solution.py:41
  169.4 1.9 fusion.112
  171.3 1.1 add_divide_fusion.1
  172.4 1.1 fusion.163
  173.5 1.9 fusion.105
  175.6 28.9 %all_to_all.47 = f32[64,4,6,128]{3,1,2,0:T(4,128)S(1)} all-to-all(f32[64,4,6,128]{3,1,2,0:T(4,128)S(1)} %copy.145), channel_id=1, replica_groups=mesh['blk'=4,'py'=8,'pz_0'=4,'pz_1'=2] {'py','pz_0','pz_1'}, dimensions={0} | all-to-all | bytes 1572864 | tf_op jit(solution)/shard_map/all_to_all | solution.py:41
  205.4 3.7 %convolution_bitcast_fusion.1 = f32[4,384,128]{2,1,0:T(8,128)S(1)} fusion(f32[4,384,128]{2,1,0:T(8,128)S(1)} %bitcast.176, s32[384]{0:T(512)S(1)} %copy-done.19, s32[384]{0:T(512)S(1)} %copy-done.22), kind=kOutput, calls=%fused_computation.8 | convolution fusion | flops 907444224 | bytes 1575936 | tf_op jit(solution)/shard_map/ypz,xp->yxz/dot_general | solution.py:181
  210.0 11.1 %all_to_all.48 = f32[4,4,65,128]{3,1,2,0:T(4,128)S(1)} all-to-all(f32[4,4,65,128]{3,1,2,0:T(4,128)S(1)} %select_select_fusion), channel_id=1, replica_groups=mesh['blk'=4,'py'=8,'pz_0'=4,'pz_1'=2] {'blk'}, dimensions={0} | all-to-all | bytes 1064960 | tf_op jit(solution)/shard_map/all_to_all | solution.py:148
  221.5 4.6 %collective-permute-start.2 = (f32[1,384,128]{2,1,0:T(8,128)S(1)}, f32[1,384,128]{2,1,0:T(8,128)S(1)}, u32[]{:S(2)}, u32[]{:S(2)}) collective-permute-start(f32[1,384,128]{2,1,0:T(8,128)S(1)} %get-tuple-element.22), channel_id=1, source_target_pairs={{0,1},{1,2},{2,3},{3,4},{4,5},{5,6},{6,7},{7,8},{8,9},{9,10},{10,1... | collective-permute-start | bytes 589832 | tf_op jit(solution)/shard_map/ppermute | solution.py:54
  226.1 1.9 collective-permute-start.3
  228.7 4.4 %collective-permute-done.3 = f32[1,384,128]{2,1,0:T(8,128)S(1)} collective-permute-done((f32[1,384,128]{2,1,0:T(8,128)S(1)}, f32[1,384,128]{2,1,0:T(8,128)S(1)}, u32[]{:S(2)}, u32[]{:S(2)}) %collective-permute-start.3) | collective-permute-done | bytes 196640 | tf_op jit(solution)/shard_map/ppermute | solution.py:56
  233.1 2.5 fusion.11
  235.6 3.7 %fusion.43 = f32[384,4,128]{2,0,1:T(8,128)S(1)} fusion(f32[4,384,128]{2,1,0:T(8,128)S(1)} %fusion.11, s32[384]{0:T(512)S(1)} %copy-done.22), kind=kOutput, calls=%fused_computation.72 | convolution fusion | flops 907444224 | bytes 1574400 | tf_op jit(solution)/shard_map/yxz,xk->ykz/dot_general | solution.py:171
  240.3 32.2 %all_to_all.49 = f32[64,4,6,128]{3,1,2,0:T(4,128)S(1)} all-to-all(f32[64,4,6,128]{3,1,2,0:T(4,128)S(1)} %copy.156), channel_id=1, replica_groups=mesh['blk'=4,'py'=8,'pz_0'=4,'pz_1'=2] {'py','pz_0','pz_1'}, dimensions={0} | all-to-all | bytes 1572864 | tf_op jit(solution)/shard_map/all_to_all | solution.py:41
  273.2 1.9 fusion.110
  275.1 1.1 add_divide_fusion
  276.2 1.1 fusion.160
  277.3 1.9 fusion.103
  280.3 5.9 %all-to-all-start.8 = ((f32[64,4,6,128]{3,1,2,0:T(4,128)}), f32[64,4,6,128]{3,1,2,0:T(4,128)S(1)}, u32[]{:S(2)}, u32[]{:S(2)}) async-start(f32[64,4,6,128]{3,1,2,0:T(4,128)} %copy.160), calls=%async_computation.8 | async-start | bytes 1572864 | tf_op jit(solution)/shard_map/all_to_all | solution.py:41
  286.2 1.8 fusion.51
  289.5 8.1 %all-reduce.4 = (f32[]{:T(128)}, f32[]{:T(128)}, f32[]{:T(128)}) all-reduce(f32[]{:T(128)} %fusion.49, f32[]{:T(128)} %fusion.50, f32[]{:T(128)} %fusion.51), channel_id=1, replica_groups=mesh['blk'=4,'py'=8,'pz_0'=4,'pz_1'=2] {'blk'}, use_global_device_ids=true, to_apply=%region_20.21 | all-reduce | flops 3 | bytes 24 | tf_op jit(solution)/shard_map/psum | solution.py:64
  297.5 16.0 %all-reduce.2 = (f32[]{:T(128)}, f32[]{:T(128)}, f32[]{:T(128)}) all-reduce(f32[]{:T(128)} %get-tuple-element.16, f32[]{:T(128)} %get-tuple-element.17, f32[]{:T(128)} %get-tuple-element.18), channel_id=1, replica_groups=mesh['blk'=4,'py'=8,'pz_0'=4,'pz_1'=2] {'py'}, use_global_device_ids=true, to_apply=%region_21.22 | all-reduce | flops 3 | bytes 24 | tf_op jit(solution)/shard_map/psum | solution.py:64
  313.5 8.4 %all-reduce.3 = (f32[]{:T(128)}, f32[]{:T(128)}, f32[]{:T(128)}) all-reduce(f32[]{:T(128)} %get-tuple-element.10, f32[]{:T(128)} %get-tuple-element.11, f32[]{:T(128)} %get-tuple-element.12), channel_id=1, replica_groups=mesh['blk'=4,'py'=8,'pz_0'=4,'pz_1'=2] {'pz_0'}, use_global_device_ids=true, to_apply=%region_22.23 | all-reduce | flops 3 | bytes 24 | tf_op jit(solution)/shard_map/psum | solution.py:64
  321.9 9.5 %all-reduce.5 = (f32[1]{0:T(128)}, f32[1]{0:T(128)}, f32[1]{0:T(128)}) all-reduce(f32[1]{0:T(128)} %bitcast.64, f32[1]{0:T(128)} %bitcast.63, f32[1]{0:T(128)} %bitcast.62), channel_id=1, replica_groups=mesh['blk'=4,'py'=8,'pz_0'=4,'pz_1'=2] {'pz_1'}, use_global_device_ids=true, to_apply=%region_23.24 | all-reduce | flops 3 | bytes 24 | tf_op jit(solution)/shard_map/psum | solution.py:64
  331.3 2.5 fusion.225
  334.7 3.7 %convolution_bitcast_fusion = f32[4,384,128]{2,1,0:T(8,128)S(1)} fusion(f32[4,384,128]{2,1,0:T(8,128)S(1)} %bitcast.174, s32[384]{0:T(512)S(1)} %copy-done.20, s32[384]{0:T(512)S(1)} %copy-done.23), kind=kOutput, calls=%fused_computation.7 | convolution fusion | flops 907444224 | bytes 1575936 | tf_op jit(solution)/shard_map/ypz,xp->yxz/dot_general | solution.py:181
  (125 shorter events, 18.3 us)
Async XLA Ops:
  0.6 6.2 %copy-start.5 = (f32[4,256,128]{2,1,0:T(8,128)S(1)}, f32[4,256,128]{2,1,0:T(8,128)}, u32[]{:S(2)}) copy-start(f32[4,256,128]{2,1,0:T(8,128)} %param.4) | copy-start | bytes 1572868
  2.8 101.3 %copy-start.6 = (pred[4]{0:T(512)(128)(4,1)}, pred[4]{0:T(512)(128)(4,1)S(1)}, u32[]{:S(2)}) copy-start(pred[4]{0:T(512)(128)(4,1)S(1)} %get-tuple-element.32) | copy-start | bytes 16
  2.8 101.3 %copy-start.8 = (pred[4]{0:T(512)(128)(4,1)}, pred[4]{0:T(512)(128)(4,1)S(1)}, u32[]{:S(2)}) copy-start(pred[4]{0:T(512)(128)(4,1)S(1)} %get-tuple-element.33) | copy-start | bytes 16
  7.0 5.9 %copy-start.17 = (s32[4,2]{0,1:T(2,128)S(1)}, s32[4,2]{0,1:T(2,128)}, u32[]{:S(2)}) copy-start(s32[4,2]{0,1:T(2,128)} %param.6) | copy-start | bytes 100
  7.9 12.6 %all-to-all-start = ((f32[4,4,64,128]{3,2,1,0:T(8,128)}), f32[4,4,64,128]{3,2,1,0:T(8,128)S(1)}, u32[]{:S(2)}, u32[]{:S(2)}) async-start(f32[4,4,64,128]{3,2,1,0:T(8,128)} %select_select_fusion.2), calls=%async_computation | async-start | bytes 1048576 | tf_op jit(solution)/shard_map/all_to_all | solution.py:128
  16.1 101.3 %copy-start.10 = (pred[4]{0:T(512)(128)(4,1)}, pred[4]{0:T(512)(128)(4,1)S(1)}, u32[]{:S(2)}) copy-start(pred[4]{0:T(512)(128)(4,1)S(1)} %get-tuple-element.37) | copy-start | bytes 16
  16.2 101.3 %copy-start.12 = (pred[4]{0:T(512)(128)(4,1)}, pred[4]{0:T(512)(128)(4,1)S(1)}, u32[]{:S(2)}) copy-start(pred[4]{0:T(512)(128)(4,1)S(1)} %get-tuple-element.38) | copy-start | bytes 16
  16.2 84.0 %copy-start.18 = (s32[384]{0:T(512)}, s32[384]{0:T(512)S(1)}, u32[]{:S(2)}) copy-start(s32[384]{0:T(512)S(1)} %get-tuple-element.41) | copy-start | bytes 4612
  16.2 84.0 %copy-start.21 = (s32[384]{0:T(512)}, s32[384]{0:T(512)S(1)}, u32[]{:S(2)}) copy-start(s32[384]{0:T(512)S(1)} %get-tuple-element.42) | copy-start | bytes 4612
  20.7 108.4 %copy-start.3 = (f32[4,64,128]{2,1,0:T(8,128)}, f32[4,64,128]{2,1,0:T(8,128)S(1)}, u32[]{:S(2)}) copy-start(f32[4,64,128]{2,1,0:T(8,128)S(1)} %get-tuple-element.7) | copy-start | bytes 393220
  20.8 3.7 %copy-start.2 = (f32[4,384,128]{2,1,0:T(8,128)}, f32[4,384,128]{2,1,0:T(8,128)S(1)}, u32[]{:S(2)}) copy-start(f32[4,384,128]{2,1,0:T(8,128)S(1)} %broadcast_multiply_fusion) | copy-start | bytes 2359300
  26.5 14.7 %copy-start.16 = (f32[3]{0:T(128)S(1)}, f32[3]{0:T(128)}, u32[]{:S(2)}) copy-start(f32[3]{0:T(128)} %param.5) | copy-start | bytes 40
  26.5 37.6 %all-to-all-start.1 = ((f32[64,4,6,128]{3,1,2,0:T(4,128)}), f32[64,4,6,128]{3,1,2,0:T(4,128)S(1)}, u32[]{:S(2)}, u32[]{:S(2)}) async-start(f32[64,4,6,128]{3,1,2,0:T(4,128)} %copy.126), calls=%async_computation.1 | async-start | bytes 1572864 | tf_op jit(solution)/shard_map/all_to_all | solution.py:41
  43.8 22.8 %copy-start.24 = (f32[128]{0:T(128)}, f32[128]{0:T(128)S(1)}, u32[]{:S(2)}) copy-start(f32[128]{0:T(128)S(1)} %multiply_multiply_fusion.1) | copy-start | bytes 1540
  44.0 22.6 %copy-start.14 = (f32[256,6]{0,1:T(8,128)}, f32[256,6]{0,1:T(8,128)S(1)}, u32[]{:S(2)}) copy-start(f32[256,6]{0,1:T(8,128)S(1)} %broadcast_add_fusion) | copy-start | bytes 18436
  103.9 4.6 %copy-start = (f32[4,384,128]{2,1,0:T(8,128)}, f32[4,384,128]{2,1,0:T(8,128)S(1)}, u32[]{:S(2)}) copy-start(f32[4,384,128]{2,1,0:T(8,128)S(1)} %convolution_bitcast_fusion.2) | copy-start | bytes 2359300
  105.0 12.4 %all-to-all-start.3 = ((f32[4,4,65,128]{3,1,2,0:T(4,128)}), f32[4,4,65,128]{3,1,2,0:T(4,128)S(1)}, u32[]{:S(2)}, u32[]{:S(2)}) async-start(f32[4,4,65,128]{3,1,2,0:T(4,128)} %select_select_fusion.1), calls=%async_computation.3 | async-start | bytes 1064960 | tf_op jit(solution)/shard_map/all_to_all | solution.py:148
  108.5 9.3 %slice-start = ((f32[4,384,128]{2,1,0:T(8,128)}), f32[4,256,128]{2,1,0:T(8,128)S(1)}, s32[]{:S(2)}) async-start(f32[4,384,128]{2,1,0:T(8,128)} %copy-done), calls=%async_computation.9 | async-start | bytes 1048576 | tf_op jit(solution)/shard_map/slice | solution.py:181
  117.9 6.8 %collective-permute-start = (f32[1,384,128]{2,1,0:T(8,128)S(1)}, f32[1,384,128]{2,1,0:T(8,128)S(1)}, u32[]{:S(2)}, u32[]{:S(2)}) collective-permute-start(f32[1,384,128]{2,1,0:T(8,128)S(1)} %get-tuple-element.24), channel_id=1, source_target_pairs={{0,1},{1,2},{2,3},{3,4},{4,5},{5,6},{6,7},{7,8},{8,9},{9,10},{10,1... | collective-permute-start | bytes 589832 | tf_op jit(solution)/shard_map/ppermute | solution.py:54
  122.1 7.0 %collective-permute-start.1 = (f32[1,384,128]{2,1,0:T(8,128)S(1)}, f32[1,384,128]{2,1,0:T(8,128)S(1)}, u32[]{:S(2)}, u32[]{:S(2)}) collective-permute-start(f32[1,384,128]{2,1,0:T(8,128)S(1)} %get-tuple-element.25), channel_id=1, source_target_pairs={{1,0},{2,1},{3,2},{4,3},{5,4},{6,5},{7,6},{8,7},{9,8},{10,9},{11,1... | collective-permute-start | bytes 589832 | tf_op jit(solution)/shard_map/ppermute | solution.py:56
  124.1 7.5 %copy-start.22 = (s32[384]{0:T(512)S(1)}, s32[384]{0:T(512)}, u32[]{:S(2)}) copy-start(s32[384]{0:T(512)} %copy-done.21) | copy-start | bytes 4612
  169.4 1.9 copy-start.15
  169.4 1.9 copy-start.25
  204.7 0.7 copy-start.19
  205.4 3.7 %copy-start.1 = (f32[4,384,128]{2,1,0:T(8,128)S(1)}, f32[4,384,128]{2,1,0:T(8,128)}, u32[]{:S(2)}) copy-start(f32[4,384,128]{2,1,0:T(8,128)} %copy-done) | copy-start | bytes 2359300
  209.2 0.6 copy-start.7
  209.2 0.6 copy-start.9
  209.8 11.2 %copy-start.11 = (pred[4]{0:T(512)(128)(4,1)S(1)}, pred[4]{0:T(512)(128)(4,1)}, u32[]{:S(2)}) copy-start(pred[4]{0:T(512)(128)(4,1)} %copy-done.10) | copy-start | bytes 16
  209.8 11.2 %copy-start.13 = (pred[4]{0:T(512)(128)(4,1)S(1)}, pred[4]{0:T(512)(128)(4,1)}, u32[]{:S(2)}) copy-start(pred[4]{0:T(512)(128)(4,1)} %copy-done.12) | copy-start | bytes 16
  221.5 11.6 %copy-start.4 = (f32[4,64,128]{2,1,0:T(8,128)S(1)}, f32[4,64,128]{2,1,0:T(8,128)}, u32[]{:S(2)}) copy-start(f32[4,64,128]{2,1,0:T(8,128)} %copy-done.3) | copy-start | bytes 393220
  221.5 7.2 %collective-permute-start.2 = (f32[1,384,128]{2,1,0:T(8,128)S(1)}, f32[1,384,128]{2,1,0:T(8,128)S(1)}, u32[]{:S(2)}, u32[]{:S(2)}) collective-permute-start(f32[1,384,128]{2,1,0:T(8,128)S(1)} %get-tuple-element.22), channel_id=1, source_target_pairs={{0,1},{1,2},{2,3},{3,4},{4,5},{5,6},{6,7},{7,8},{8,9},{9,10},{10,1... | collective-permute-start | bytes 589832 | tf_op jit(solution)/shard_map/ppermute | solution.py:54
  226.1 7.0 %collective-permute-start.3 = (f32[1,384,128]{2,1,0:T(8,128)S(1)}, f32[1,384,128]{2,1,0:T(8,128)S(1)}, u32[]{:S(2)}, u32[]{:S(2)}) collective-permute-start(f32[1,384,128]{2,1,0:T(8,128)S(1)} %get-tuple-element.23), channel_id=1, source_target_pairs={{1,0},{2,1},{3,2},{4,3},{5,4},{6,5},{7,6},{8,7},{9,8},{10,9},{11,1... | collective-permute-start | bytes 589832 | tf_op jit(solution)/shard_map/ppermute | solution.py:56
  280.3 53.5 %all-to-all-start.8 = ((f32[64,4,6,128]{3,1,2,0:T(4,128)}), f32[64,4,6,128]{3,1,2,0:T(4,128)S(1)}, u32[]{:S(2)}, u32[]{:S(2)}) async-start(f32[64,4,6,128]{3,1,2,0:T(4,128)} %copy.160), calls=%async_computation.8 | async-start | bytes 1572864 | tf_op jit(solution)/shard_map/all_to_all | solution.py:41
  334.0 0.7 copy-start.20
  334.1 0.7 copy-start.23
where the time goes:
time: 346 us; the launch traced here: 340 us
  blocking collectives  175 us (51%)
  waiting for transfers between devices  43.2 us (12%)
  starting transfers between devices  41.7 us (12%)
  matrix products  40.1 us (12%)
  other arithmetic  19.1 us (6%)
  local copies, waits for them, and re-layouts  14.7 us (4%)
  between operations  5.64 us (2%)
    all_to_all x4, blocking collectives, one_exchange(): lax.all_to_all(blocks, axis, split_axis=0, concat_axis=0, tiled=True)  122 us
    psum x4, blocking collectives, one_axis_at_a_time(): return functools.reduce(lax.psum, axes, x)  41.9 us
    all_to_all x2, starting transfers between devices, one_exchange(): lax.all_to_all(blocks, axis, split_axis=0, concat_axis=0, tiled=True)  20.6 us
    all_to_all x2, waiting for transfers between devices, one_exchange(): lax.all_to_all(blocks, axis, split_axis=0, concat_axis=0, tiled=True)  20 us
    dot_general x3, matrix products, shards(): modes = jnp.einsum('yxz,xk->ykz', residual, plane_basis, precision=HIGHEST)  11.1 us
    all_to_all x1, blocking collectives, shards(): lax.all_to_all(outgoing(iterate[:, :OV + 1, :], iterate[:, BX - OV - 1:,...  11.1 us
    dot_general x3, matrix products, shards(): jnp.einsum('ypz,xp->yxz', returned, plane_back, precision=HIGHEST)  11 us
    all_to_all x1, waiting for transfers between devices, shards(): lax.all_to_all(outgoing(iterate[:, :OV + 1, :], iterate[:, BX - OV - 1:,...  8.91 us
  transfers between devices with their start and end apart: 8, of which 7 were waited for; matrix products, arithmetic and copies ran while one was open for 3% of the time, Pallas kernels for 0%

commit v1 on v0

v1 whole, which is shorter than its diff:
```python
import functools

import jax
import jax.numpy as jnp
import ml_dtypes
import numpy as np
from jax import lax
from jax.experimental import pallas as pl
from jax.experimental.pallas import tpu as pltpu
from jax.sharding import PartitionSpec as P

NY = 256
NZ = 128
BX = 256
OV = 64
EXT = 384
BLOCKS = 4
PY = 8
PZ = 8
PLANE = PY * PZ
ROWS = NY // PLANE
HALVES = 2
MODES = 256
MESH = pl.DeviceIdType.MESH
F32 = jnp.float32
BF16 = jnp.bfloat16
NN = (((1,), (0,)), ((), ()))
NT = (((1,), (1,)), ((), ()))
CELLS = float(BLOCKS * BX * NY * NZ)


def basis(n):
    j = np.arange(1, n + 1)
    m = (j[:, None] * j[None, :]) % (2 * (n + 1))
    return np.sqrt(2.0 / (n + 1)) * np.sin(np.pi * m / (n + 1))


def eigenvalues(n):
    return 4.0 * np.sin(np.pi * np.arange(1, n + 1) / (2.0 * (n + 1))) ** 2


def halves(a):
    a = a.astype(np.float32)
    hi = a.astype(ml_dtypes.bfloat16)
    lo = (a - hi.astype(np.float32)).astype(ml_dtypes.bfloat16)
    return np.stack([hi, lo])


@functools.lru_cache(None)
def tables():
    depth = basis(NZ)
    rows = basis(NY)
    planes = basis(EXT)
    margin = basis(OV)
    order = (ROWS * np.arange(PLANE)[None, :] + np.arange(ROWS)[:, None]).reshape(-1)
    rows_in = rows[:, order]
    ends = np.zeros((2 * OV, BX))
    ends[:OV, :OV] = margin[0][:, None] * margin.T
    ends[OV:, BX - OV :] = margin[OV - 1][:, None] * margin.T
    planes_in = planes[OV : OV + BX].T
    four = np.zeros((8, EXT))
    four[:4] = planes[[OV - 1, OV, OV + BX - 1, OV + BX]]
    lanes = np.ones((1, 128))
    return (
        halves(depth),
        halves(rows_in),
        halves(rows_in.T),
        halves(np.concatenate([planes_in, ends], axis=0)),
        halves(planes_in.T),
        halves(four),
        halves(four.T),
        (eigenvalues(EXT)[:, None] * lanes).astype(np.float32),
        (eigenvalues(OV)[:, None] * lanes).astype(np.float32),
        eigenvalues(NY)[None, :].astype(np.float32),
    )


def split(x):
    hi = x.astype(BF16)
    return hi, (x - hi.astype(F32)).astype(BF16)


def times(table, x, dims):
    hi, lo = split(x)
    dot = functools.partial(lax.dot_general, dimension_numbers=dims, preferred_element_type=F32)
    return dot(table[0], hi) + (dot(table[0], lo) + dot(table[1], hi))


def times_right(x, table, dims):
    hi, lo = split(x)
    dot = functools.partial(lax.dot_general, dimension_numbers=dims, preferred_element_type=F32)
    return dot(hi, table[0]) + (dot(lo, table[0]) + dot(hi, table[1]))


def kernel(
    source,
    conduct,
    neighbours,
    orient,
    depth_spectrum,
    *refs,
):
    consts_hbm = refs[:10]
    out, norms = refs[10:12]
    consts = refs[12:22]
    (
        src,
        sent,
        got,
        modes,
        inverse,
        inverse_margin,
        ends_out,
        ends_in,
        back,
        returned,
        result,
        norm_out,
        norm_x,
        norm_mid,
        norm_z,
        src_sem,
        const_sem,
        out_sem,
        go_send,
        go_recv,
        ends_send,
        ends_recv,
        back_send,
        back_recv,
        norm_send,
        norm_recv,
    ) = refs[22:]
    depth, rows_in, rows_out, planes_in, planes_out, four_in, four_out, mu_planes, mu_margin, mu_rows = consts

    blk = lax.axis_index("blk")
    py = lax.axis_index("py")
    pz = lax.axis_index("pz")
    place = py * PZ + pz

    def peer(step):
        to_py = lax.rem(py + lax.rem(step, PY), PY)
        to_pz = lax.rem(pz + step // PY, PZ)
        return to_py, to_pz, to_py * PZ + to_pz

    barrier = pltpu.get_barrier_semaphore()

    def greet(step, carry):
        to_py, to_pz, _ = peer(step)
        pl.semaphore_signal(barrier, inc=1, device_id=(blk, to_py, to_pz), device_id_type=MESH)
        return carry

    loads = [pltpu.make_async_copy(source.at[y], src.at[y], src_sem.at[y]) for y in range(ROWS)]
    fetches = [pltpu.make_async_copy(a, b, const_sem.at[i]) for i, (a, b) in enumerate(zip(consts_hbm, consts))]
    fetches[0].start()
    for load in loads:
        load.start()
    lax.fori_loop(1, PLANE, greet, 0)
    for step in range(1, BLOCKS):
        pl.semaphore_signal(
            barrier, inc=1, device_id=(lax.rem(blk + step, BLOCKS), py, pz), device_id_type=MESH
        )
    for fetch in fetches[1:]:
        fetch.start()

    fetches[0].wait()
    squares = jnp.zeros((8, 128), F32)
    for y in range(ROWS):
        loads[y].wait()
        cells = src[y]
        squares = squares + jnp.sum((cells * cells).reshape(BX // 8, 8, NZ), axis=0)
        z = times((depth[0], depth[1]), cells, NT)
        for h in range(HALVES):
            for x in range(2):
                sent[h, pl.ds(4 * x + y, PLANE, stride=8), :] = z[
                    PLANE * h : PLANE * (h + 1), 128 * x : 128 * (x + 1)
                ]
    own_squares = jnp.sum(jnp.sum(squares, axis=0, keepdims=True), axis=1, keepdims=True)

    pl.semaphore_wait(barrier, PLANE - 1 + BLOCKS - 1)

    def tile(d):
        return pl.ds(pl.multiple_of(d * 8, 8), 8)

    def exchange(src_ref, dst_ref, send_sem, recv_sem, h):
        def send(step, carry):
            to_py, to_pz, to = peer(step)
            pltpu.make_async_remote_copy(
                src_ref=src_ref.at[h, tile(to), :],
                dst_ref=dst_ref.at[h, tile(place), :],
                send_sem=send_sem.at[h],
                recv_sem=recv_sem.at[h],
                device_id=(blk, to_py, to_pz),
                device_id_type=MESH,
            ).start()
            return carry

        lax.fori_loop(1, PLANE, send, 0)
        dst_ref[h, tile(place), :] = src_ref[h, tile(place), :]

    def all_of(src_ref, dst_ref, send_sem, recv_sem, h):
        others = pl.ds(0, (PLANE - 1) * 8)
        return pltpu.make_async_remote_copy(
            src_ref=src_ref.at[h, others, :],
            dst_ref=dst_ref.at[h, others, :],
            send_sem=send_sem.at[h],
            recv_sem=recv_sem.at[h],
            device_id=(blk, lax.rem(py + 1, PY), pz),
            device_id_type=MESH,
        )

    for h in range(HALVES):
        exchange(sent, got, go_send, go_recv, h)

    for fetch in fetches[1:]:
        fetch.wait()

    c0 = conduct[0]
    c1 = conduct[1]
    c2 = conduct[2]

    order = [jnp.int32(0)]
    for b in range(BLOCKS):
        order[0] = order[0] + b * (neighbours[b, 0] == -1).astype(jnp.int32)
    for m in range(1, BLOCKS):
        following = jnp.int32(0)
        for b in range(BLOCKS):
            following = following + neighbours[b, 1] * (order[m - 1] == b).astype(jnp.int32)
        order.append(following)
    is_at = [[(order[m] == b).astype(F32) for b in range(BLOCKS)] for m in range(BLOCKS)]
    own_at = [(order[m] == blk).astype(F32) for m in range(BLOCKS)]
    block_flips = [(orient[b] == 1).astype(F32) for b in range(BLOCKS)]
    flips = [sum(is_at[m][b] * block_flips[b] for b in range(BLOCKS)) for m in range(BLOCKS)]
    own_flip = sum(own_at[m] * flips[m] for m in range(BLOCKS))

    row_id = lax.broadcasted_iota(jnp.int32, (8, MODES), 0)

    def pick(flag, yes, no):
        return yes * flag + no * (1.0 - flag)

    greens = []
    for h in range(HALVES):
        shift = c1 * mu_rows[...] + c2 * depth_spectrum[PLANE * h + place]
        inverse[h] = 1.0 / (c0 * jnp.concatenate([mu_planes[...]] * 2, axis=1) + shift)
        inverse_margin[h] = 1.0 / (c0 * jnp.concatenate([mu_margin[...]] * 2, axis=1) + shift)
        half = jnp.sqrt(shift / (4.0 * c0))
        square = half * half
        theta = 2.0 * jnp.log1p(half + square / (1.0 + jnp.sqrt(1.0 + square)))

        def power(n):
            return jnp.exp(-n * theta)

        def fall(n):
            return 1.0 - power(2.0 * n)

        scale = 1.0 / (fall(1.0) * fall(385.0))
        f64, f65, f320, f321 = fall(64.0), fall(65.0), fall(320.0), fall(321.0)
        table = {
            (0, 0): power(1.0) * f64 * f321 * scale,
            (0, 1): power(2.0) * f64 * f320 * scale,
            (0, 2): power(257.0) * f64 * f65 * scale,
            (0, 3): power(258.0) * f64 * f64 * scale,
            (1, 1): power(1.0) * f65 * f320 * scale,
            (1, 2): power(256.0) * f65 * f65 * scale,
        }
        for a, b, c, d in ((1, 3, 0, 2), (2, 2, 1, 1), (2, 3, 0, 1), (3, 3, 0, 0)):
            table[a, b] = table[c, d]
        for a in range(4):
            for b in range(a):
                table[a, b] = table[b, a]
        greens.append((table, jnp.exp(theta) * f65 / f64))

    def to_ends(h, step):
        return pltpu.make_async_remote_copy(
            src_ref=ends_out.at[h],
            dst_ref=ends_in.at[h, blk],
            send_sem=ends_send.at[h, step - 1],
            recv_sem=ends_recv.at[h, step - 1],
            device_id=(lax.rem(blk + step, BLOCKS), py, pz),
            device_id_type=MESH,
        )

    def assembled(ref, h, r):
        return jnp.concatenate(
            [ref[h, pl.ds(4 * x + r, PLANE, stride=8), :] for x in range(2)], axis=1
        )

    for h in range(HALVES):
        all_of(sent, got, go_send, go_recv, h).wait_recv()
        plane = jnp.concatenate([assembled(got, h, r) for r in range(ROWS)], axis=0)
        hat = times((rows_in[0], rows_in[1]), plane, NN)
        both = times((planes_in[0], planes_in[1]), hat, NT)
        held = both[:EXT]
        modes[h] = held
        near = times((four_in[0], four_in[1]), held * inverse[h], NN)
        margins = both[EXT:]
        ratio = greens[h][1]
        low = jnp.sum(margins[:OV] * inverse_margin[h], axis=0, keepdims=True) * ratio
        high = jnp.sum(margins[OV:] * inverse_margin[h], axis=0, keepdims=True) * ratio
        near = (
            near
            + jnp.where(row_id == 4, low, 0.0)
            + jnp.where(row_id == 5, high, 0.0)
            + jnp.where(row_id == 6, own_squares, 0.0)
        )
        ends_out[h] = near
        ends_in[h, blk] = near
        for step in range(1, BLOCKS):
            to_ends(h, step).start()

    change_1 = jnp.zeros((1, MODES), F32)
    change_2 = jnp.zeros((1, MODES), F32)
    total_squares = jnp.zeros((1, 1), F32)
    for h in range(HALVES):
        for step in range(1, BLOCKS):
            to_ends(h, step).wait_recv()
        table = greens[h][0]
        tiles = [ends_in[h, b] for b in range(BLOCKS)]
        if h == 0:
            for b in range(BLOCKS):
                total_squares = total_squares + tiles[b][6:7, :1]
        base, low, high = [], [], []
        for m in range(BLOCKS):
            at = sum(tiles[b] * is_at[m][b] for b in range(BLOCKS))
            row = [at[i : i + 1] for i in range(6)]
            base.append([pick(flips[m], row[3 - p], row[p]) for p in range(4)])
            low.append(pick(flips[m], row[5], row[4]))
            high.append(pick(flips[m], row[4], row[5]))
        zero = jnp.zeros((1, MODES), F32)
        outer = [
            [high[m - 1] if m > 0 else zero, zero, zero, low[m + 1] if m < BLOCKS - 1 else zero]
            for m in range(BLOCKS)
        ]

        def solved(m, p, sources):
            return base[m][p] + sum(table[p, q] * sources[m][q] for q in range(4))

        def jumps(sources):
            last = BLOCKS - 1
            left = [solved(m + 1, 1, sources) - solved(m, 3, sources) for m in range(last)]
            left.append(-solved(last, 3, sources))
            right = [solved(m, 2, sources) - solved(m + 1, 0, sources) for m in range(last)]
            right.append(-solved(0, 0, sources))
            return left, right

        def with_jumps(left, right):
            result = [list(o) for o in outer]
            for m in range(BLOCKS - 1):
                result[m][2] = left[m]
                result[m][3] = outer[m][3] + right[m]
                result[m + 1][1] = right[m]
                result[m + 1][0] = outer[m + 1][0] + left[m]
            result[BLOCKS - 1][2] = left[BLOCKS - 1]
            result[0][1] = right[BLOCKS - 1]
            return result

        left_1, right_1 = jumps(outer)
        left_2, right_2 = jumps(with_jumps(left_1, right_1))
        for a, b in zip(left_1 + right_1, left_2 + right_2):
            change_1 = change_1 + a * a
            change_2 = change_2 + (b - a) * (b - a)
        final = with_jumps(left_2, right_2)
        own = [sum(own_at[m] * final[m][p] for m in range(BLOCKS)) for p in range(4)]
        own = [pick(own_flip, own[3 - p], own[p]) for p in range(4)]
        added = sum(jnp.where(row_id == p, own[p] * c0, 0.0) for p in range(4))
        solution_modes = inverse[h] * (modes[h] + times((four_out[0], four_out[1]), added, NN))
        across = times((planes_out[0], planes_out[1]), solution_modes, NN)
        plane = times((rows_out[0], rows_out[1]), across, NT)
        for r in range(ROWS):
            for x in range(2):
                back[h, pl.ds(4 * x + r, PLANE, stride=8), :] = plane[
                    PLANE * r : PLANE * (r + 1), 128 * x : 128 * (x + 1)
                ]
        exchange(back, returned, back_send, back_recv, h)

    lane = lax.broadcasted_iota(jnp.int32, (1, 128), 1)

    def total(x):
        return jnp.sum(x, axis=1, keepdims=True)

    partial = (
        jnp.where(lane == 0, total_squares, 0.0)
        + jnp.where(lane == 1, total(change_1) * (c0 * c0), 0.0)
        + jnp.where(lane == 2, total(change_2) * (c0 * c0), 0.0)
    )

    def norm_copy(src_ref, dst_ref, stage, step):
        device = (
            (blk, py, lax.rem(pz + step, PZ)) if stage == 0 else (blk, lax.rem(py + step, PY), pz)
        )
        return pltpu.make_async_remote_copy(
            src_ref=src_ref,
            dst_ref=dst_ref.at[pz if stage == 0 else py],
            send_sem=norm_send.at[stage, step - 1],
            recv_sem=norm_recv.at[stage, step - 1],
            device_id=device,
            device_id_type=MESH,
        )

    norm_out[...] = partial
    norm_x[pz] = partial
    for step in range(1, PZ):
        norm_copy(norm_out, norm_x, 0, step).start()
    for step in range(1, PZ):
        norm_copy(norm_out, norm_x, 0, step).wait_recv()
    partial = sum(norm_x[i] for i in range(PZ))
    norm_mid[...] = partial
    norm_z[py] = partial
    for step in range(1, PY):
        norm_copy(norm_mid, norm_z, 1, step).start()

    for h in range(HALVES):
        all_of(back, returned, back_send, back_recv, h).wait_recv()
    for r in range(ROWS):
        stacked = jnp.concatenate([assembled(returned, h, r) for h in range(HALVES)], axis=0)
        result[r] = times_right(stacked.T, (depth[0], depth[1]), NN)
        pltpu.make_async_copy(result.at[r], out.at[r], out_sem.at[r]).start()

    for step in range(1, PY):
        norm_copy(norm_mid, norm_z, 1, step).wait_recv()
    partial = jnp.sqrt(sum(norm_z[i] for i in range(PY)) / CELLS)
    for i in range(3):
        norms[i] = jnp.sum(jnp.where(lane == i, partial, 0.0))

    for h in range(HALVES):
        all_of(sent, got, go_send, go_recv, h).wait_send()
        all_of(back, returned, back_send, back_recv, h).wait_send()
        for step in range(1, BLOCKS):
            to_ends(h, step).wait_send()
    for step in range(1, PZ):
        norm_copy(norm_out, norm_x, 0, step).wait_send()
        norm_copy(norm_mid, norm_z, 1, step).wait_send()
    for r in range(ROWS):
        pltpu.make_async_copy(result.at[r], out.at[r], out_sem.at[r]).wait()


def shards(source, conduct, neighbours, orient):
    consts = tables()
    any_space = pl.BlockSpec(memory_space=pl.ANY)
    smem = pl.BlockSpec(memory_space=pltpu.SMEM)
    dma = pltpu.SemaphoreType.DMA
    chunked = pltpu.VMEM((HALVES, PLANE * 8, 128), F32)
    return pl.pallas_call(
        kernel,
        name="schwarz",
        out_shape=(
            jax.ShapeDtypeStruct((ROWS, BX, NZ), F32),
            jax.ShapeDtypeStruct((3,), F32),
        ),
        in_specs=[any_space, smem, smem, smem, smem] + [any_space] * len(consts),
        out_specs=(any_space, smem),
        scratch_shapes=[pltpu.VMEM(c.shape, c.dtype) for c in consts]
        + [
            pltpu.VMEM((ROWS, BX, NZ), F32),
            chunked,
            chunked,
            pltpu.VMEM((HALVES, EXT, MODES), F32),
            pltpu.VMEM((HALVES, EXT, MODES), F32),
            pltpu.VMEM((HALVES, OV, MODES), F32),
            pltpu.VMEM((HALVES, 8, MODES), F32),
            pltpu.VMEM((HALVES, BLOCKS, 8, MODES), F32),
            chunked,
            chunked,
            pltpu.VMEM((ROWS, BX, NZ), F32),
            pltpu.VMEM((1, 128), F32),
            pltpu.VMEM((PZ, 1, 128), F32),
            pltpu.VMEM((1, 128), F32),
            pltpu.VMEM((PY, 1, 128), F32),
            dma((ROWS,)),
            dma((len(consts),)),
            dma((ROWS,)),
            dma((HALVES,)),
            dma((HALVES,)),
            dma((HALVES, BLOCKS - 1)),
            dma((HALVES, BLOCKS - 1)),
            dma((HALVES,)),
            dma((HALVES,)),
            dma((2, PZ - 1)),
            dma((2, PZ - 1)),
        ],
        compiler_params=pltpu.CompilerParams(collective_id=0, has_side_effects=True),
    )(
        source,
        conduct,
        neighbours,
        orient,
        jnp.asarray(eigenvalues(NZ).astype(np.float32)),
        *[jnp.asarray(c) for c in consts],
    )


def solution(mesh):
    cells = P(("py", "pz"), "blk", None)
    return jax.shard_map(
        shards, mesh=mesh, in_specs=(cells, P(), P(), P()), out_specs=(cells, P()), check_vma=False
    )
```

time: 346 us -> 51.3 us (0.15); the launches traced: 340 us -> 51.1 us
  blocking collectives: 175 us -> 0 us
  Pallas kernels: 0 us -> 46.8 us
  waiting for transfers between devices: 43.2 us -> 0 us
  starting transfers between devices: 41.7 us -> 0 us
  matrix products: 40.1 us -> 0 us
  other arithmetic: 19.1 us -> 0 us
  local copies, waits for them, and re-layouts: 14.7 us -> 3.72 us
  between operations: 5.64 us -> 0.65 us
    all_to_all x5 -> x0, blocking collectives: 134 us -> none  [the longest x4 122 us: one_exchange(): lax.all_to_all(blocks, axis, split_axis=0, concat_axis=0, tiled=True)]
    pallas_call x0 -> x1, Pallas kernels: none -> 46.8 us  [shards(): pl.pallas_call(kernel, name='schwarz', out_shape=(jax.ShapeDtypeStruct((R...]
    psum x4 -> x0, blocking collectives: 41.9 us -> none  [one_axis_at_a_time(): return functools.reduce(lax.psum, axes, x)]
    dot_general x18 -> x0, matrix products: 40.1 us -> none  [the longest x3 11.1 us: shards(): modes = jnp.einsum('yxz,xk->ykz', residual, plane_basis, precision=HIGHEST)]
    all_to_all x4 -> x0, waiting for transfers between devices: 33.3 us -> none  [the longest x2 20 us: one_exchange(): lax.all_to_all(blocks, axis, split_axis=0, concat_axis=0, tiled=True)]
    all_to_all x4 -> x0, starting transfers between devices: 29.1 us -> none  [the longest x2 20.6 us: one_exchange(): lax.all_to_all(blocks, axis, split_axis=0, concat_axis=0, tiled=True)]
    ppermute x4 -> x0, starting transfers between devices: 12.6 us -> none  [the longest x2 8.76 us: extended_2(): lax.ppermute(tail, axis, [(i, (i + 1) % count) for i in range(ends)])]
    ppermute x4 -> x0, waiting for transfers between devices: 9.98 us -> none  [the longest x2 8.79 us: extended_2(): lax.ppermute(head, axis, [((i + 1) % count, i) for i in range(ends)])]
  transfers between devices with their start and end apart: 8 -> 0, of which waited for: 7 -> 0; matrix products, arithmetic and copies ran while one was open for 3% -> 0% of each run, Pallas kernels for 0% -> 0%
where the time goes in v1:
time: 51.3 us; the launch traced here: 51.1 us
  Pallas kernels  46.8 us (91%)
  local copies, waits for them, and re-layouts  3.72 us (7%)
  between operations  0.65 us (1%)
    pallas_call x1, Pallas kernels, shards(): pl.pallas_call(kernel, name='schwarz', out_shape=(jax.ShapeDtypeStruct((R...  46.8 us
    unnamed x5, local copies, waits for them, and re-layouts  3.72 us

profile of v1, /device:TPU:1, one launch (start us, length us, event | category | flops | bytes accessed | tf_op | source)
XLA Modules:
  0.0 51.1 jit_solution(12898100160709756955)
XLA Ops:
  0.6 1.3 %copy.17.neighbours = s32[4,2]{1,0:T(4,128)} copy(s32[4,2]{0,1:T(2,128)} %param.17) | data formatting | bytes 64 | tf_op args[2]
  2.0 46.8 %schwarz.1 = (f32[4,256,128]{2,1,0:T(8,128)}, f32[3]{0:T(128)}) custom-call(f32[4,256,128]{2,1,0:T(8,128)} %source.1, f32[3]{0:T(128)} %conduct.1, s32[4,2]{1,0:T(4,128)} %copy.17.neighbours, s32[4]{0:T(128)} %orient.1, f32[128]{0:T(128)} %constant.22.clone.depth_spectrum, bf16[2,128,128]{2,1,0:T(8,128)(2,1)} %constant.23.clone.refs_0_, ...), custom_call_target="tpu_custom_call" | custom-call | tf_op jit(solution)/shard_map/schwarz/pallas_call | solution.py:443
  48.7 0.0 copy-start
  48.8 1.9 %copy.20 = f32[4,256,128]{2,1,0:T(8,128)} copy(f32[4,256,128]{2,1,0:T(8,128)} %get-tuple-element.4) | data formatting | bytes 1048576
  50.6 0.0 copy-done
  50.6 0.5 %copy.21 = f32[3]{0:T(128)} copy(f32[3]{0:T(128)S(1)} %copy-done) | data formatting | bytes 24
Async XLA Ops:
  48.7 1.9 %copy-start = (f32[3]{0:T(128)S(1)}, f32[3]{0:T(128)}, u32[]{:S(2)}) copy-start(f32[3]{0:T(128)} %get-tuple-element.5) | copy-start | bytes 40

commit v2 on v1

v2 whole, which is shorter than its diff:
```python
import functools

import jax
import jax.numpy as jnp
import ml_dtypes
import numpy as np
from jax import lax
from jax.experimental import pallas as pl
from jax.experimental.pallas import tpu as pltpu
from jax.sharding import PartitionSpec as P

NY = 256
NZ = 128
BX = 256
OV = 64
EXT = 384
BLOCKS = 4
PY = 8
PZ = 8
PLANE = PY * PZ
ROWS = NY // PLANE
HALVES = 2
MODES = 256
MESH = pl.DeviceIdType.MESH
F32 = jnp.float32
BF16 = jnp.bfloat16
NN = (((1,), (0,)), ((), ()))
NT = (((1,), (1,)), ((), ()))
CELLS = float(BLOCKS * BX * NY * NZ)
TN = (((0,), (0,)), ((), ()))


def basis(n):
    j = np.arange(1, n + 1)
    m = (j[:, None] * j[None, :]) % (2 * (n + 1))
    return np.sqrt(2.0 / (n + 1)) * np.sin(np.pi * m / (n + 1))


def eigenvalues(n):
    return 4.0 * np.sin(np.pi * np.arange(1, n + 1) / (2.0 * (n + 1))) ** 2


def halves(a):
    a = a.astype(np.float32)
    hi = a.astype(ml_dtypes.bfloat16)
    lo = (a - hi.astype(np.float32)).astype(ml_dtypes.bfloat16)
    return np.stack([hi, lo])


@functools.lru_cache(None)
def tables():
    depth = halves(basis(NZ))
    rows = basis(NY)
    planes = basis(EXT)
    order = (ROWS * np.arange(PLANE)[None, :] + np.arange(ROWS)[:, None]).reshape(-1)
    planes_in = planes[OV : OV + BX].T
    depth_in = np.concatenate([depth[0], depth[0], depth[1]], axis=1)
    depth_out = np.stack(
        [
            np.concatenate([part[PLANE * h : PLANE * (h + 1)] for part in (depth[0], depth[0], depth[1])], axis=0)
            for h in range(HALVES)
        ]
    )
    return (
        depth_in,
        halves(rows[order]),
        halves(rows[order]),
        halves(planes_in),
        halves(planes_in.T),
        (eigenvalues(EXT)[:, None] * np.ones((1, 128))).astype(np.float32),
        eigenvalues(NY)[None, :].astype(np.float32),
        depth_out,
    )


def split(x):
    hi = x.astype(BF16)
    return hi, (x - hi.astype(F32)).astype(BF16)


def dot(a, b, dims):
    return lax.dot_general(a, b, dimension_numbers=dims, preferred_element_type=F32)


def times(table, x, dims):
    hi, lo = split(x)
    return dot(table[0], hi, dims) + (dot(table[0], lo, dims) + dot(table[1], hi, dims))


def times_right(x, table, dims):
    hi, lo = split(x)
    return dot(hi, table[0], dims) + (dot(lo, table[0], dims) + dot(hi, table[1], dims))


def assembled(ref, h, r):
    return jnp.concatenate([ref[h, pl.ds(4 * x + r, PLANE, stride=8), :] for x in range(2)], axis=1)


def depth_back(ref, h, r, table):
    hi, lo = split(assembled(ref, h, r))
    return dot(jnp.concatenate([hi, lo, hi], axis=0), table[h], TN)


def kernel(source, conduct_hbm, neighbours_hbm, orient_hbm, spectrum_hbm, *refs):
    consts_hbm = refs[:8]
    returned, partial_out, norm_z, depth_out = refs[8:12]
    consts = refs[12:19] + (depth_out,)
    (
        conduct,
        neighbours,
        orient,
        depth_spectrum,
        src,
        sent,
        got,
        base,
        inverse,
        toward_low,
        toward_high,
        margin_low,
        margin_high,
        ends_out,
        ends_in,
        back,
        norm_out,
        norm_x,
        norm_mid,
        src_sem,
        const_sem,
        small_sem,
        go_send,
        go_recv,
        ends_send,
        ends_recv,
        back_send,
        back_recv,
        norm_send,
        norm_recv,
    ) = refs[19:]
    depth_in, rows_in, rows_out, planes_in, planes_out, mu_planes, mu_rows, _ = consts

    blk = lax.axis_index("blk")
    py = lax.axis_index("py")
    pz = lax.axis_index("pz")
    place = py * PZ + pz

    def wrapped(a, n):
        return jnp.where(a >= n, a - n, a)

    def peer(step):
        to_py = wrapped(py + step % PY, PY)
        to_pz = wrapped(pz + step // PY, PZ)
        return to_py, to_pz, to_py * PZ + to_pz

    def everyone(visit):
        def one(near, to_pz):
            to_py = wrapped(py + near, PY)
            visit(to_py, to_pz, to_py * PZ + to_pz)

        def column(far, carry):
            to_pz = wrapped(pz + far, PZ)
            for near in range(PY):
                one(near, to_pz)
            return carry

        for near in range(1, PY):
            one(near, pz)
        lax.fori_loop(1, PZ, column, 0)

    barrier = pltpu.get_barrier_semaphore()

    def greet(to_py, to_pz, to):
        pl.semaphore_signal(barrier, inc=1, device_id=(blk, to_py, to_pz), device_id_type=MESH)

    loads = [pltpu.make_async_copy(source.at[y], src.at[y], src_sem.at[y]) for y in range(ROWS)]
    fetches = [pltpu.make_async_copy(a, b, const_sem.at[i]) for i, (a, b) in enumerate(zip(consts_hbm, consts))]
    smalls = [
        pltpu.make_async_copy(a, b, small_sem.at[i])
        for i, (a, b) in enumerate(
            (
                (conduct_hbm, conduct),
                (neighbours_hbm, neighbours),
                (orient_hbm, orient),
                (spectrum_hbm, depth_spectrum),
            )
        )
    ]
    fetches[0].start()
    for load in loads:
        load.start()
    everyone(greet)
    for step in range(1, BLOCKS):
        pl.semaphore_signal(
            barrier, inc=1, device_id=(wrapped(blk + step, BLOCKS), py, pz), device_id_type=MESH
        )
    for small in smalls:
        small.start()
    for fetch in fetches[1:]:
        fetch.start()

    fetches[0].wait()
    squares = jnp.zeros((8, 128), F32)
    for y in range(ROWS):
        loads[y].wait()
        cells = src[y]
        squares = squares + jnp.sum((cells * cells).reshape(BX // 8, 8, NZ), axis=0)
        hi, lo = split(cells)
        z = dot(depth_in[...], jnp.concatenate([hi, lo, hi], axis=1), NT)
        for h in range(HALVES):
            for x in range(2):
                sent[h, pl.ds(4 * x + y, PLANE, stride=8), :] = z[
                    PLANE * h : PLANE * (h + 1), 128 * x : 128 * (x + 1)
                ]
    own_squares = jnp.sum(jnp.sum(squares, axis=0, keepdims=True), axis=1, keepdims=True)

    pl.semaphore_wait(barrier, PLANE - 1 + BLOCKS - 1)

    def tile(d):
        return pl.ds(pl.multiple_of(d * 8, 8), 8)

    def exchange(src_ref, dst_ref, send_sem, recv_sem, h):
        def send(to_py, to_pz, to):
            pltpu.make_async_remote_copy(
                src_ref=src_ref.at[h, tile(to), :],
                dst_ref=dst_ref.at[h, tile(place), :],
                send_sem=send_sem.at[h],
                recv_sem=recv_sem.at[h],
                device_id=(blk, to_py, to_pz),
                device_id_type=MESH,
            ).start()

        everyone(send)
        dst_ref[h, tile(place), :] = src_ref[h, tile(place), :]

    def all_of(src_ref, dst_ref, send_sem, recv_sem, h):
        others = pl.ds(0, (PLANE - 1) * 8)
        return pltpu.make_async_remote_copy(
            src_ref=src_ref.at[h, others, :],
            dst_ref=dst_ref.at[h, others, :],
            send_sem=send_sem.at[h],
            recv_sem=recv_sem.at[h],
            device_id=(blk, wrapped(py + 1, PY), pz),
            device_id_type=MESH,
        )

    for h in range(HALVES):
        exchange(sent, got, go_send, go_recv, h)

    for wait in smalls + fetches[1:]:
        wait.wait()

    c0 = conduct[0]
    c1 = conduct[1]
    c2 = conduct[2]

    order = [jnp.int32(0)]
    for b in range(BLOCKS):
        order[0] = order[0] + b * (neighbours[0, b] == -1).astype(jnp.int32)
    for m in range(1, BLOCKS):
        following = jnp.int32(0)
        for b in range(BLOCKS):
            following = following + neighbours[1, b] * (order[m - 1] == b).astype(jnp.int32)
        order.append(following)
    is_at = [[(order[m] == b).astype(F32) for b in range(BLOCKS)] for m in range(BLOCKS)]
    own_at = [(order[m] == blk).astype(F32) for m in range(BLOCKS)]
    block_flips = [(orient[b] == 1).astype(F32) for b in range(BLOCKS)]
    flips = [sum(is_at[m][b] * block_flips[b] for b in range(BLOCKS)) for m in range(BLOCKS)]
    own_flip = sum(own_at[m] * flips[m] for m in range(BLOCKS))

    row_id = lax.broadcasted_iota(jnp.int32, (8, MODES), 0)

    def pick(flag, yes, no):
        return yes * flag + no * (1.0 - flag)

    plane_id = lax.broadcasted_iota(jnp.int32, (BX, MODES), 0).astype(F32)
    margin_id = lax.broadcasted_iota(jnp.int32, (OV, MODES), 0).astype(F32)
    greens = []
    for h in range(HALVES):
        shift = c1 * mu_rows[...] + c2 * depth_spectrum[PLANE * h + place]
        inverse[h] = 1.0 / (c0 * jnp.concatenate([mu_planes[...]] * 2, axis=1) + shift)
        half = jnp.sqrt(shift / (4.0 * c0))
        square = half * half
        theta = 2.0 * jnp.log1p(half + square / (1.0 + jnp.sqrt(1.0 + square)))

        def power(n):
            return jnp.exp(-n * theta)

        def fall(n):
            return 1.0 - power(2.0 * n)

        scale = 1.0 / (fall(1.0) * fall(385.0))
        f64, f65, f320, f321 = fall(64.0), fall(65.0), fall(320.0), fall(321.0)
        table = {
            (0, 0): power(1.0) * f64 * f321 * scale,
            (0, 1): power(2.0) * f64 * f320 * scale,
            (0, 2): power(257.0) * f64 * f65 * scale,
            (0, 3): power(258.0) * f64 * f64 * scale,
            (1, 1): power(1.0) * f65 * f320 * scale,
            (1, 2): power(256.0) * f65 * f65 * scale,
        }
        for a, b, c, d in ((1, 3, 0, 2), (2, 2, 1, 1), (2, 3, 0, 1), (3, 3, 0, 0)):
            table[a, b] = table[c, d]
        for a in range(4):
            for b in range(a):
                table[a, b] = table[b, a]
        greens.append((table, jnp.exp(theta) * f65 / f64))
        rise = jnp.exp(-plane_id * theta)
        drop = jnp.exp((plane_id - float(BX)) * theta)
        edge = f64 * scale
        far_low = drop * power(64.0)
        far_high = rise * power(65.0)
        toward_low[h] = rise * (power(2.0) * edge) * (1.0 - far_low * far_low)
        toward_high[h] = drop * (power(1.0) * edge) * (1.0 - far_high * far_high)
        inside = jnp.exp((margin_id - float(OV)) * theta)
        margin_low[h] = jnp.exp(-margin_id * theta) * ((1.0 - inside * inside) / f64)
        outside = jnp.exp(-(margin_id + 1.0) * theta)
        margin_high[h] = jnp.exp((margin_id - float(OV - 1)) * theta) * ((1.0 - outside * outside) / f64)

    def to_ends(h, step):
        return pltpu.make_async_remote_copy(
            src_ref=ends_out.at[h],
            dst_ref=ends_in.at[h, blk],
            send_sem=ends_send.at[h, step - 1],
            recv_sem=ends_recv.at[h, step - 1],
            device_id=(wrapped(blk + step, BLOCKS), py, pz),
            device_id_type=MESH,
        )

    def summed(x):
        return jnp.sum(x, axis=0, keepdims=True)

    lane = lax.broadcasted_iota(jnp.int32, (1, 128), 1)

    def total(x):
        return jnp.sum(x, axis=1, keepdims=True)

    def norm_copy(src_ref, dst_ref, stage, step):
        device = (blk, py, wrapped(pz + step, PZ)) if stage == 0 else (blk, wrapped(py + step, PY), pz)
        return pltpu.make_async_remote_copy(
            src_ref=src_ref,
            dst_ref=dst_ref.at[pz if stage == 0 else py],
            send_sem=norm_send.at[stage, step - 1],
            recv_sem=norm_recv.at[stage, step - 1],
            device_id=device,
            device_id_type=MESH,
        )

    change_1 = jnp.zeros((1, MODES), F32)
    change_2 = jnp.zeros((1, MODES), F32)
    total_squares = jnp.zeros((1, 1), F32)
    zero = jnp.zeros((1, MODES), F32)
    for h in range(HALVES):
        table, ratio = greens[h]
        all_of(sent, got, go_send, go_recv, h).wait_recv()
        plane = jnp.concatenate([assembled(got, h, r) for r in range(ROWS)], axis=0)
        held = times_right(plane.T, (rows_in[0], rows_in[1]), NN)
        near = (
            jnp.where(row_id == 0, summed(held * toward_low[h]) * (1.0 / c0), 0.0)
            + jnp.where(row_id == 1, summed(held * toward_high[h]) * (1.0 / c0), 0.0)
            + jnp.where(row_id == 2, summed(held[:OV] * margin_low[h]) * (1.0 / c0), 0.0)
            + jnp.where(row_id == 3, summed(held[BX - OV :] * margin_high[h]) * (1.0 / c0), 0.0)
            + jnp.where(row_id == 4, own_squares, 0.0)
        )
        ends_out[h] = near
        ends_in[h, blk] = near
        for step in range(1, BLOCKS):
            to_ends(h, step).start()

        solved_modes = times((planes_in[0], planes_in[1]), held, NN) * inverse[h]
        base[h] = times((planes_out[0], planes_out[1]), solved_modes, NN)

        for step in range(1, BLOCKS):
            to_ends(h, step).wait_recv()
        tiles = [ends_in[h, b] for b in range(BLOCKS)]
        if h == 0:
            for b in range(BLOCKS):
                total_squares = total_squares + tiles[b][4:5, :1]
        first, low, high = [], [], []
        for m in range(BLOCKS):
            at = sum(tiles[b] * is_at[m][b] for b in range(BLOCKS))
            left = pick(flips[m], at[1:2], at[0:1])
            right = pick(flips[m], at[0:1], at[1:2])
            first.append([left, left * ratio, right * ratio, right])
            low.append(pick(flips[m], at[3:4], at[2:3]))
            high.append(pick(flips[m], at[2:3], at[3:4]))
        outer = [
            [high[m - 1] if m > 0 else zero, zero, zero, low[m + 1] if m < BLOCKS - 1 else zero]
            for m in range(BLOCKS)
        ]

        def solved(m, p, sources):
            return first[m][p] + sum(table[p, q] * sources[m][q] for q in range(4))

        def jumps(sources):
            last = BLOCKS - 1
            left = [solved(m + 1, 1, sources) - solved(m, 3, sources) for m in range(last)]
            left.append(-solved(last, 3, sources))
            right = [solved(m, 2, sources) - solved(m + 1, 0, sources) for m in range(last)]
            right.append(-solved(0, 0, sources))
            return left, right

        def with_jumps(left, right):
            result = [list(o) for o in outer]
            for m in range(BLOCKS - 1):
                result[m][2] = left[m]
                result[m][3] = outer[m][3] + right[m]
                result[m + 1][1] = right[m]
                result[m + 1][0] = outer[m + 1][0] + left[m]
            result[BLOCKS - 1][2] = left[BLOCKS - 1]
            result[0][1] = right[BLOCKS - 1]
            return result

        left_1, right_1 = jumps(outer)
        left_2, right_2 = jumps(with_jumps(left_1, right_1))
        for a, b in zip(left_1 + right_1, left_2 + right_2):
            change_1 = change_1 + a * a
            change_2 = change_2 + (b - a) * (b - a)
        final = with_jumps(left_2, right_2)
        at_low = sum(own_at[m] * (final[m][0] + ratio * final[m][1]) for m in range(BLOCKS))
        at_high = sum(own_at[m] * (final[m][3] + ratio * final[m][2]) for m in range(BLOCKS))
        at_low, at_high = pick(own_flip, at_high, at_low), pick(own_flip, at_low, at_high)

        if h == HALVES - 1:
            partial = (
                jnp.where(lane == 0, total_squares, 0.0)
                + jnp.where(lane == 1, total(change_1) * (c0 * c0), 0.0)
                + jnp.where(lane == 2, total(change_2) * (c0 * c0), 0.0)
            )
            norm_out[...] = partial
            norm_x[pz] = partial
            for step in range(1, PZ):
                norm_copy(norm_out, norm_x, 0, step).start()

        across = base[h] + toward_low[h] * at_low + toward_high[h] * at_high
        plane = times((rows_out[0], rows_out[1]), across, NT)
        for r in range(ROWS):
            for x in range(2):
                back[h, pl.ds(4 * x + r, PLANE, stride=8), :] = plane[
                    PLANE * r : PLANE * (r + 1), 128 * x : 128 * (x + 1)
                ]
        exchange(back, returned, back_send, back_recv, h)

    for step in range(1, PZ):
        norm_copy(norm_out, norm_x, 0, step).wait_recv()
    partial = sum(norm_x[i] for i in range(PZ))
    norm_mid[...] = partial
    norm_z[py] = partial
    for step in range(1, PY):
        norm_copy(norm_mid, norm_z, 1, step).start()

    all_of(back, returned, back_send, back_recv, 0).wait_recv()
    for r in range(ROWS):
        partial_out[r] = depth_back(returned, 0, r, depth_out)

    for h in range(HALVES):
        all_of(sent, got, go_send, go_recv, h).wait_send()
        for step in range(1, BLOCKS):
            to_ends(h, step).wait_send()
    for step in range(1, PZ):
        norm_copy(norm_out, norm_x, 0, step).wait_send()
    all_of(back, returned, back_send, back_recv, 0).wait_send()
    all_of(back, returned, back_send, back_recv, 1).wait_recv()
    for step in range(1, PY):
        norm_copy(norm_mid, norm_z, 1, step).wait_recv()
    all_of(back, returned, back_send, back_recv, 1).wait_send()
    for step in range(1, PY):
        norm_copy(norm_mid, norm_z, 1, step).wait_send()


def finish(returned, partial_out, norm_z, depth_out, out, norms, result, out_sem):
    copies = []
    for r in range(ROWS):
        result[r] = partial_out[r] + depth_back(returned, 1, r, depth_out)
        copies.append(pltpu.make_async_copy(result.at[r], out.at[r], out_sem.at[r]))
        copies[r].start()
    lane = lax.broadcasted_iota(jnp.int32, (1, 128), 1)
    root = jnp.sqrt(sum(norm_z[i] for i in range(PY)) / CELLS)
    for i in range(3):
        norms[i] = jnp.sum(jnp.where(lane == i, root, 0.0))
    for copy in copies:
        copy.wait()


def shards(source, conduct, neighbours, orient):
    consts = tables()
    any_space = pl.BlockSpec(memory_space=pltpu.HBM)
    smem = pl.BlockSpec(memory_space=pltpu.SMEM)
    vmem = pl.BlockSpec(memory_space=pltpu.VMEM)
    dma = pltpu.SemaphoreType.DMA
    chunked = (HALVES, PLANE * 8, 128)
    cells = pltpu.VMEM((ROWS, BX, NZ), F32)
    limit = 24 * 1024 * 1024
    handed = pl.pallas_call(
        kernel,
        name="schwarz",
        out_shape=(
            jax.ShapeDtypeStruct(chunked, F32),
            jax.ShapeDtypeStruct((ROWS, BX, NZ), F32),
            jax.ShapeDtypeStruct((PY, 1, 128), F32),
            jax.ShapeDtypeStruct(consts[-1].shape, BF16),
        ),
        in_specs=[any_space] * (5 + len(consts)),
        out_specs=(vmem,) * 4,
        scratch_shapes=[pltpu.VMEM(c.shape, c.dtype) for c in consts[:-1]]
        + [
            pltpu.SMEM((3,), F32),
            pltpu.SMEM((2, BLOCKS), jnp.int32),
            pltpu.SMEM((BLOCKS,), jnp.int32),
            pltpu.SMEM((NZ,), F32),
            cells,
            pltpu.VMEM(chunked, F32),
            pltpu.VMEM(chunked, F32),
            pltpu.VMEM((HALVES, BX, MODES), F32),
            pltpu.VMEM((HALVES, EXT, MODES), F32),
            pltpu.VMEM((HALVES, BX, MODES), F32),
            pltpu.VMEM((HALVES, BX, MODES), F32),
            pltpu.VMEM((HALVES, OV, MODES), F32),
            pltpu.VMEM((HALVES, OV, MODES), F32),
            pltpu.VMEM((HALVES, 8, MODES), F32),
            pltpu.VMEM((HALVES, BLOCKS, 8, MODES), F32),
            pltpu.VMEM(chunked, F32),
            pltpu.VMEM((1, 128), F32),
            pltpu.VMEM((PZ, 1, 128), F32),
            pltpu.VMEM((1, 128), F32),
            dma((ROWS,)),
            dma((len(consts),)),
            dma((4,)),
            dma((HALVES,)),
            dma((HALVES,)),
            dma((HALVES, BLOCKS - 1)),
            dma((HALVES, BLOCKS - 1)),
            dma((HALVES,)),
            dma((HALVES,)),
            dma((2, PZ - 1)),
            dma((2, PZ - 1)),
        ],
        compiler_params=pltpu.CompilerParams(collective_id=0, has_side_effects=True, vmem_limit_bytes=limit),
    )(
        *[
            pltpu.with_memory_space_constraint(jnp.asarray(a), pltpu.HBM)
            for a in (
                source,
                conduct,
                neighbours.T,
                orient,
                eigenvalues(NZ).astype(np.float32),
                *consts,
            )
        ]
    )
    return pl.pallas_call(
        finish,
        name="finish",
        out_shape=(
            jax.ShapeDtypeStruct((ROWS, BX, NZ), F32),
            jax.ShapeDtypeStruct((3,), F32),
        ),
        in_specs=[vmem] * 4,
        out_specs=(any_space, smem),
        scratch_shapes=[cells, dma((ROWS,))],
        compiler_params=pltpu.CompilerParams(vmem_limit_bytes=limit),
    )(*handed)


def solution(mesh):
    cells = P(("py", "pz"), "blk", None)
    return jax.shard_map(
        shards, mesh=mesh, in_specs=(cells, P(), P(), P()), out_specs=(cells, P()), check_vma=False
    )
```

time: 51.3 us -> 44.5 us (0.87)
  local copies, waits for them, and re-layouts: 3.72 us -> 0 us
  Pallas kernels: 46.8 us -> 43.7 us
    unnamed x5 -> x0, local copies, waits for them, and re-layouts: 3.72 us -> none
    pallas_call x1 -> x2, Pallas kernels: 46.8 us -> 43.7 us  [the longest x1 42.1 us: shards(): pl.pallas_call(kernel, name='schwarz', out_shape=(jax.ShapeDtypeStruct(ch...]
where the time goes in v2:
time: 44.5 us; the launch traced here: 44.4 us
  Pallas kernels  43.7 us (98%)
  between operations  0.64 us (1%)
    pallas_call x1, Pallas kernels, shards(): pl.pallas_call(kernel, name='schwarz', out_shape=(jax.ShapeDtypeStruct(ch...  42.1 us
    pallas_call x1, Pallas kernels, shards(): pl.pallas_call(finish, name='finish', out_shape=(jax.ShapeDtypeStruct((RO...  1.59 us

profile of v2, /device:TPU:1, one launch (start us, length us, event | category | flops | bytes accessed | tf_op | source)
XLA Modules:
  0.0 44.4 jit_solution(1352050325024393056)
XLA Ops:
  0.6 42.1 %schwarz.1 = (f32[2,512,128]{2,1,0:T(8,128)S(1)}, f32[4,256,128]{2,1,0:T(8,128)S(1)}, f32[8,1,128]{2,1,0:T(1,128)S(1)}, bf16[2,192,128]{2,1,0:T(8,128)(2,1)S(1)}) custom-call(f32[4,256,128]{2,1,0:T(8,128)} %source.1, f32[3]{0:T(128)} %conduct_hbm.1, s32[2,4]{1,0:T(2,128)} %bitcast.1, s32[4]{0:T(128)} %orient_hbm.1, f32[128]{0:T(128)} %constant.16.clone.spectrum_hbm, ...), custom_call_target="tpu_custom_call" | custom-call | tf_op jit(solution)/shard_map/schwarz/pallas_call | solution.py:493
  42.8 1.6 %finish.1 = (f32[4,256,128]{2,1,0:T(8,128)}, f32[3]{0:T(128)}) custom-call(f32[2,512,128]{2,1,0:T(8,128)S(1)} %get-tuple-element.6.returned, f32[4,256,128]{2,1,0:T(8,128)S(1)} %get-tuple-element.7.partial_out, f32[8,1,128]{2,1,0:T(1,128)S(1)} %get-tuple-element.8.norm_z, bf16[2,192,128]{2,1,0:T(8,128)(2,1)S(1)} %get-tuple-element.9.depth_out), custom_call_target="tpu_custom_call" | custom-call | tf_op jit(solution)/shard_map/finish/pallas_call | solution.py:551

commit v3 on v2

--- a/solution.py
+++ b/solution.py
@@ -28,6 +28,9 @@
 NT = (((1,), (1,)), ((), ()))
 CELLS = float(BLOCKS * BX * NY * NZ)
 TN = (((0,), (0,)), ((), ()))
+SLOTS = 5
+CONSTS = 13
+EARLY = 3
 
 
 def basis(n):
@@ -52,7 +55,16 @@
     depth = halves(basis(NZ))
     rows = basis(NY)
     planes = basis(EXT)
-    order = (ROWS * np.arange(PLANE)[None, :] + np.arange(ROWS)[:, None]).reshape(-1)
+    first = ROWS * np.arange(PLANE)
+    outer_rows = rows[np.concatenate([first, first + ROWS - 1])]
+    inner_rows = np.concatenate([rows[first + 1], rows[first + 2]], axis=1)
+    inner = np.zeros((BX, BX))
+    inner[1:-1, :-2] = basis(BX - 2)
+    mu_inner = np.concatenate([eigenvalues(BX - 2), np.ones(2)])[None, :]
+    rims = np.zeros((128, 2 * BX))
+    rims[:4] = np.concatenate(
+        [np.stack([inner[1], inner[-2]] * 2), np.stack([inner[1], inner[-2], -inner[1], -inner[-2]])], axis=1
+    )
     planes_in = planes[OV : OV + BX].T
     depth_in = np.concatenate([depth[0], depth[0], depth[1]], axis=1)
     depth_out = np.stack(
@@ -63,12 +75,17 @@
     )
     return (
         depth_in,
-        halves(rows[order]),
-        halves(rows[order]),
+        mu_inner.astype(np.float32),
+        (eigenvalues(NZ)[:, None] * np.ones((1, 128))).astype(np.float32),
+        halves(outer_rows),
+        halves(inner_rows),
         halves(planes_in),
         halves(planes_in.T),
         (eigenvalues(EXT)[:, None] * np.ones((1, 128))).astype(np.float32),
         eigenvalues(NY)[None, :].astype(np.float32),
+        halves(inner),
+        halves(inner.T),
+        halves(rims),
         depth_out,
     )
 
@@ -92,19 +109,48 @@
     return dot(hi, table[0], dims) + (dot(lo, table[0], dims) + dot(hi, table[1], dims))
 
 
-def assembled(ref, h, r):
-    return jnp.concatenate([ref[h, pl.ds(4 * x + r, PLANE, stride=8), :] for x in range(2)], axis=1)
-
-
-def depth_back(ref, h, r, table):
-    hi, lo = split(assembled(ref, h, r))
-    return dot(jnp.concatenate([hi, lo, hi], axis=0), table[h], TN)
+def row_of(ref, h, slot):
+    return ref[h, pl.ds(slot, PLANE, stride=SLOTS), :]
+
+
+def outer_row(ref, h, r):
+    return jnp.concatenate([row_of(ref, h, 2 * r + x) for x in range(2)], axis=1)
+
+
+def restored(returned, h, local, by_row, by_plane, inner, inner_back, rims, depth_out):
+    low_row = outer_row(returned, h, 0)
+    high_row = outer_row(returned, h, 1)
+    rim = row_of(returned, h, 4)
+    from_rows = times_right(
+        jnp.concatenate([low_row + high_row, low_row - high_row], axis=0), (inner[0], inner[1]), NN
+    )
+    from_rim = times_right(rim, (rims[0], rims[1]), NN)
+    from_rim = jnp.concatenate([from_rim[:, :BX], from_rim[:, BX:]], axis=0)
+    both = times_right(
+        local[h] + by_row[h] * from_rows + by_plane[h] * from_rim, (inner_back[0], inner_back[1]), NN
+    )
+    plane = lax.broadcasted_iota(jnp.int32, (PLANE, BX), 1)
+
+    def edged(cells, slot):
+        cells = jnp.where(plane == 0, rim[:, slot : slot + 1], cells)
+        return jnp.where(plane == BX - 1, rim[:, slot + 1 : slot + 2], cells)
+
+    even, odd = both[:PLANE], both[PLANE:]
+    rows = (low_row, edged(even + odd, 0), edged(even - odd, 2), high_row)
+    return [depth_back(cells, depth_out[h]) for cells in rows]
+
+
+def depth_back(cells, table):
+    hi, lo = split(cells)
+    return dot(jnp.concatenate([hi, lo, hi], axis=0), table, TN)
 
 
 def kernel(source, conduct_hbm, neighbours_hbm, orient_hbm, spectrum_hbm, *refs):
-    consts_hbm = refs[:8]
-    returned, partial_out, norm_z, depth_out = refs[8:12]
-    consts = refs[12:19] + (depth_out,)
+    consts_hbm = refs[:CONSTS]
+    returned, partial_out, norm_z, local, by_row, by_plane, inner, inner_back, rims, depth_out = refs[
+        CONSTS : CONSTS + 10
+    ]
+    consts = refs[CONSTS + 10 : 2 * CONSTS + 6] + (inner, inner_back, rims, depth_out)
     (
         conduct,
         neighbours,
@@ -136,8 +182,8 @@
         back_recv,
         norm_send,
         norm_recv,
-    ) = refs[19:]
-    depth_in, rows_in, rows_out, planes_in, planes_out, mu_planes, mu_rows, _ = consts
+    ) = refs[2 * CONSTS + 6 :]
+    depth_in, mu_inner, mu_depth, outer_rows, inner_rows, planes_in, planes_out, mu_planes, mu_rows = consts[:9]
 
     blk = lax.axis_index("blk")
     py = lax.axis_index("py")
@@ -185,38 +231,72 @@
             )
         )
     ]
-    fetches[0].start()
-    for load in loads:
-        load.start()
+    early = fetches[:EARLY] + fetches[9:11]
+    late = fetches[EARLY:9] + fetches[11:]
+    for start in smalls + loads + early:
+        start.start()
     everyone(greet)
     for step in range(1, BLOCKS):
         pl.semaphore_signal(
             barrier, inc=1, device_id=(wrapped(blk + step, BLOCKS), py, pz), device_id_type=MESH
         )
-    for small in smalls:
-        small.start()
-    for fetch in fetches[1:]:
+    for fetch in late:
         fetch.start()
 
     fetches[0].wait()
     squares = jnp.zeros((8, 128), F32)
+    rows = []
     for y in range(ROWS):
         loads[y].wait()
         cells = src[y]
         squares = squares + jnp.sum((cells * cells).reshape(BX // 8, 8, NZ), axis=0)
         hi, lo = split(cells)
-        z = dot(depth_in[...], jnp.concatenate([hi, lo, hi], axis=1), NT)
-        for h in range(HALVES):
+        rows.append(dot(depth_in[...], jnp.concatenate([hi, lo, hi], axis=1), NT))
+    own_squares = jnp.sum(jnp.sum(squares, axis=0, keepdims=True), axis=1, keepdims=True)
+
+    for wait in smalls + early[1:]:
+        wait.wait()
+    c0 = conduct[0]
+    c1 = conduct[1]
+    c2 = conduct[2]
+
+    base_part = c0 * mu_inner[...] + c2 * jnp.concatenate([mu_depth[...]] * 2, axis=1)
+    weights = jnp.concatenate([0.5 / (base_part + c1), 0.5 / (base_part + 3.0 * c1)], axis=0)
+    mixed = jnp.concatenate([rows[1] + rows[2], rows[1] - rows[2]], axis=0)
+    inner_modes = times_right(mixed, (inner[0], inner[1]), NN) * weights
+    for h in range(HALVES):
+        own = [slice(NZ * q + PLANE * h, NZ * q + PLANE * (h + 1)) for q in range(2)]
+        weight = jnp.concatenate([weights[part] for part in own], axis=0)
+        local[h] = jnp.concatenate([inner_modes[part] for part in own], axis=0)
+        by_row[h] = weight * c1
+        by_plane[h] = weight * c0
+    both = times_right(inner_modes, (inner_back[0], inner_back[1]), NN)
+    solved_rows = (both[:NZ] + both[NZ:], both[:NZ] - both[NZ:])
+    lanes = lax.broadcasted_iota(jnp.int32, (NZ, 128), 1)
+    rim = jnp.zeros((NZ, 128), F32)
+    for r in range(2):
+        near, far = solved_rows[r][:, :128], solved_rows[r][:, 128:]
+        at_first = rows[1 + r][:, :128] + c0 * pltpu.roll(near, 127, 1)
+        at_last = rows[1 + r][:, 128:] + c0 * pltpu.roll(far, 1, 1)
+        part = jnp.where(lanes == 0, at_first, 0.0)
+        part = jnp.where(lanes == 127, at_last, part)
+        part = jnp.where(lanes == OV, near, part)
+        part = jnp.where(lanes == OV - 1, far, part)
+        rim = rim + (part if r == 0 else pltpu.roll(part, 2, 1))
+    outer_cells = (rows[0] + c1 * solved_rows[0], rows[3] + c1 * solved_rows[1])
+    for h in range(HALVES):
+        part = slice(PLANE * h, PLANE * (h + 1))
+        for r in range(2):
             for x in range(2):
-                sent[h, pl.ds(4 * x + y, PLANE, stride=8), :] = z[
-                    PLANE * h : PLANE * (h + 1), 128 * x : 128 * (x + 1)
+                sent[h, pl.ds(2 * r + x, PLANE, stride=SLOTS), :] = outer_cells[r][
+                    part, 128 * x : 128 * (x + 1)
                 ]
-    own_squares = jnp.sum(jnp.sum(squares, axis=0, keepdims=True), axis=1, keepdims=True)
+        sent[h, pl.ds(4, PLANE, stride=SLOTS), :] = rim[part]
 
     pl.semaphore_wait(barrier, PLANE - 1 + BLOCKS - 1)
 
     def tile(d):
-        return pl.ds(pl.multiple_of(d * 8, 8), 8)
+        return pl.ds(d * SLOTS, SLOTS)
 
     def exchange(src_ref, dst_ref, send_sem, recv_sem, h):
         def send(to_py, to_pz, to):
@@ -233,7 +313,7 @@
         dst_ref[h, tile(place), :] = src_ref[h, tile(place), :]
 
     def all_of(src_ref, dst_ref, send_sem, recv_sem, h):
-        others = pl.ds(0, (PLANE - 1) * 8)
+        others = pl.ds(0, (PLANE - 1) * SLOTS)
         return pltpu.make_async_remote_copy(
             src_ref=src_ref.at[h, others, :],
             dst_ref=dst_ref.at[h, others, :],
@@ -246,12 +326,8 @@
     for h in range(HALVES):
         exchange(sent, got, go_send, go_recv, h)
 
-    for wait in smalls + fetches[1:]:
-        wait.wait()
-
-    c0 = conduct[0]
-    c1 = conduct[1]
-    c2 = conduct[2]
+    for fetch in late:
+        fetch.wait()
 
     order = [jnp.int32(0)]
     for b in range(BLOCKS):
@@ -352,13 +428,27 @@
     for h in range(HALVES):
         table, ratio = greens[h]
         all_of(sent, got, go_send, go_recv, h).wait_recv()
-        plane = jnp.concatenate([assembled(got, h, r) for r in range(ROWS)], axis=0)
-        held = times_right(plane.T, (rows_in[0], rows_in[1]), NN)
+        plane = jnp.concatenate([outer_row(got, h, r) for r in range(2)], axis=0)
+        held = times_right(plane.T, (outer_rows[0], outer_rows[1]), NN)
+        extra = times_right(row_of(got, h, 4).T, (inner_rows[0], inner_rows[1]), NN)
+        one, two = extra[:, :MODES], extra[:, MODES:]
+        at_first = one[0:1] + two[2:3]
+        at_last = one[127:128] + two[1:2]
+        cut_low = (one[OV : OV + 1] + two[OV + 2 : OV + 3]) * c0
+        cut_high = (one[OV - 1 : OV] + two[OV + 1 : OV + 2]) * c0
+        held = jnp.concatenate(
+            [
+                held[:8] + jnp.where(row_id == 0, at_first, 0.0),
+                held[8:-8],
+                held[-8:] + jnp.where(row_id == 7, at_last, 0.0),
+            ],
+            axis=0,
+        )
         near = (
             jnp.where(row_id == 0, summed(held * toward_low[h]) * (1.0 / c0), 0.0)
             + jnp.where(row_id == 1, summed(held * toward_high[h]) * (1.0 / c0), 0.0)
-            + jnp.where(row_id == 2, summed(held[:OV] * margin_low[h]) * (1.0 / c0), 0.0)
-            + jnp.where(row_id == 3, summed(held[BX - OV :] * margin_high[h]) * (1.0 / c0), 0.0)
+            + jnp.where(row_id == 2, (summed(held[:OV] * margin_low[h]) - cut_low * margin_low[h, OV - 1 : OV, :]) * (1.0 / c0), 0.0)
+            + jnp.where(row_id == 3, (summed(held[BX - OV :] * margin_high[h]) - cut_high * margin_high[h, 0:1, :]) * (1.0 / c0), 0.0)
             + jnp.where(row_id == 4, own_squares, 0.0)
         )
         ends_out[h] = near
@@ -432,12 +522,22 @@
                 norm_copy(norm_out, norm_x, 0, step).start()
 
         across = base[h] + toward_low[h] * at_low + toward_high[h] * at_high
-        plane = times((rows_out[0], rows_out[1]), across, NT)
-        for r in range(ROWS):
+        plane = times((outer_rows[0], outer_rows[1]), across, NT)
+        ends = [across[:1], across[-1:]]
+        rim_modes = jnp.concatenate(
+            [
+                sum(jnp.where(row_id == 2 * r + e, ends[e], 0.0) for e in range(2))
+                for r in range(2)
+            ],
+            axis=1,
+        )
+        rim_modes = jnp.concatenate([rim_modes, jnp.zeros((120, 2 * MODES), F32)], axis=0)
+        for r in range(2):
             for x in range(2):
-                back[h, pl.ds(4 * x + r, PLANE, stride=8), :] = plane[
+                back[h, pl.ds(2 * r + x, PLANE, stride=SLOTS), :] = plane[
                     PLANE * r : PLANE * (r + 1), 128 * x : 128 * (x + 1)
                 ]
+        back[h, pl.ds(4, PLANE, stride=SLOTS), :] = times((inner_rows[0], inner_rows[1]), rim_modes, NT)
         exchange(back, returned, back_send, back_recv, h)
 
     for step in range(1, PZ):
@@ -449,8 +549,10 @@
         norm_copy(norm_mid, norm_z, 1, step).start()
 
     all_of(back, returned, back_send, back_recv, 0).wait_recv()
-    for r in range(ROWS):
-        partial_out[r] = depth_back(returned, 0, r, depth_out)
+    for r, cells in enumerate(
+        restored(returned, 0, local, by_row, by_plane, inner, inner_back, rims, depth_out)
+    ):
+        partial_out[r] = cells
 
     for h in range(HALVES):
         all_of(sent, got, go_send, go_recv, h).wait_send()
@@ -467,10 +569,11 @@
         norm_copy(norm_mid, norm_z, 1, step).wait_send()
 
 
-def finish(returned, partial_out, norm_z, depth_out, out, norms, result, out_sem):
+def finish(returned, partial_out, norm_z, *refs):
+    held, (out, norms, result, out_sem) = refs[:-4], refs[-4:]
     copies = []
-    for r in range(ROWS):
-        result[r] = partial_out[r] + depth_back(returned, 1, r, depth_out)
+    for r, cells in enumerate(restored(returned, 1, *held)):
+        result[r] = partial_out[r] + cells
         copies.append(pltpu.make_async_copy(result.at[r], out.at[r], out_sem.at[r]))
         copies[r].start()
     lane = lax.broadcasted_iota(jnp.int32, (1, 128), 1)
@@ -487,7 +590,8 @@
     smem = pl.BlockSpec(memory_space=pltpu.SMEM)
     vmem = pl.BlockSpec(memory_space=pltpu.VMEM)
     dma = pltpu.SemaphoreType.DMA
-    chunked = (HALVES, PLANE * 8, 128)
+    chunked = (HALVES, PLANE * SLOTS, 128)
+    modal = (HALVES, 2 * PLANE, BX)
     cells = pltpu.VMEM((ROWS, BX, NZ), F32)
     limit = 24 * 1024 * 1024
     handed = pl.pallas_call(
@@ -497,11 +601,14 @@
             jax.ShapeDtypeStruct(chunked, F32),
             jax.ShapeDtypeStruct((ROWS, BX, NZ), F32),
             jax.ShapeDtypeStruct((PY, 1, 128), F32),
-            jax.ShapeDtypeStruct(consts[-1].shape, BF16),
+            jax.ShapeDtypeStruct(modal, F32),
+            jax.ShapeDtypeStruct(modal, F32),
+            jax.ShapeDtypeStruct(modal, F32),
+            *[jax.ShapeDtypeStruct(c.shape, BF16) for c in consts[-4:]],
         ),
         in_specs=[any_space] * (5 + len(consts)),
-        out_specs=(vmem,) * 4,
-        scratch_shapes=[pltpu.VMEM(c.shape, c.dtype) for c in consts[:-1]]
+        out_specs=(vmem,) * 10,
+        scratch_shapes=[pltpu.VMEM(c.shape, c.dtype) for c in consts[:-4]]
         + [
             pltpu.SMEM((3,), F32),
             pltpu.SMEM((2, BLOCKS), jnp.int32),
@@ -555,7 +662,7 @@
             jax.ShapeDtypeStruct((ROWS, BX, NZ), F32),
             jax.ShapeDtypeStruct((3,), F32),
         ),
-        in_specs=[vmem] * 4,
+        in_specs=[vmem] * 10,
         out_specs=(any_space, smem),
         scratch_shapes=[cells, dma((ROWS,))],
         compiler_params=pltpu.CompilerParams(vmem_limit_bytes=limit),

time: 44.5 us -> 40.1 us (0.901)
  Pallas kernels: 43.7 us -> 39.4 us
    pallas_call x1, Pallas kernels: 42.1 us -> 37.3 us  [shards(): pl.pallas_call(kernel, name='schwarz', out_shape=(jax.ShapeDtypeStruct(ch...]
where the time goes in v3:
time: 40.1 us; the launch traced here: 40 us
  Pallas kernels  39.4 us (98%)
  between operations  0.64 us (2%)
    pallas_call x1, Pallas kernels, shards(): pl.pallas_call(kernel, name='schwarz', out_shape=(jax.ShapeDtypeStruct(ch...  37.3 us
    pallas_call x1, Pallas kernels, shards(): pl.pallas_call(finish, name='finish', out_shape=(jax.ShapeDtypeStruct((RO...  2.03 us

profile of v3, /device:TPU:1, one launch (start us, length us, event | category | flops | bytes accessed | tf_op | source)
XLA Modules:
  0.0 40.0 jit_solution(16922421588676863407)
XLA Ops:
  0.6 37.3 %schwarz.1 = (f32[2,320,128]{2,1,0:T(8,128)S(1)}, f32[4,256,128]{2,1,0:T(8,128)S(1)}, f32[8,1,128]{2,1,0:T(1,128)S(1)}, f32[2,128,256]{2,1,0:T(8,128)S(1)}, f32[...) custom-call(f32[4,256,128]{2,1,0:T(8,128)} %source.1, ...), custom_call_target="tpu_custom_call" | custom-call | tf_op jit(solution)/shard_map/schwarz/pallas_call | solution.py:597
  38.0 2.0 %finish.1 = (f32[4,256,128]{2,1,0:T(8,128)}, f32[3]{0:T(128)}) custom-call(f32[2,320,128]{2,1,0:T(8,128)S(1)} %get-tuple-element.12.returned, f32[4,256,128]{2,1,0:T(8,128)S(1)} %get-tuple-element.13.partial_out, f32[8,1,128]{2,1,0:T(1,128)S(1)} %get-tuple-element.14.norm_z, f32[2,128,256]{2,1,0:T(8,128)S(1)} %get-tuple-element.15.refs_0_, ...), custom_call_target="tpu_custom_call" | custom-call | tf_op jit(solution)/shard_map/finish/pallas_call | solution.py:658

commit v4 on v3

--- a/solution.py
+++ b/solution.py
@@ -28,7 +28,8 @@
 NT = (((1,), (1,)), ((), ()))
 CELLS = float(BLOCKS * BX * NY * NZ)
 TN = (((0,), (0,)), ((), ()))
-SLOTS = 5
+BACK = 5
+THERE = (5, 4)
 CONSTS = 13
 EARLY = 3
 
@@ -109,18 +110,20 @@
     return dot(hi, table[0], dims) + (dot(lo, table[0], dims) + dot(hi, table[1], dims))
 
 
-def row_of(ref, h, slot):
-    return ref[h, pl.ds(slot, PLANE, stride=SLOTS), :]
-
-
-def outer_row(ref, h, r):
-    return jnp.concatenate([row_of(ref, h, 2 * r + x) for x in range(2)], axis=1)
+def row_of(ref, h, slot, slots):
+    return ref[h, pl.ds(slot, PLANE, stride=slots), :]
+
+
+def outer_row(ref, h, r, slots):
+    return jnp.concatenate([row_of(ref, h, 2 * r + x, slots) for x in range(2)], axis=1)
 
 
 def restored(returned, h, local, by_row, by_plane, inner, inner_back, rims, depth_out):
-    low_row = outer_row(returned, h, 0)
-    high_row = outer_row(returned, h, 1)
-    rim = row_of(returned, h, 4)
+    low_row = outer_row(returned, h, 0, BACK)
+    high_row = outer_row(returned, h, 1, BACK)
+    yield 0, depth_back(low_row, depth_out[h])
+    yield 3, depth_back(high_row, depth_out[h])
+    rim = row_of(returned, h, 4, BACK)
     from_rows = times_right(
         jnp.concatenate([low_row + high_row, low_row - high_row], axis=0), (inner[0], inner[1]), NN
     )
@@ -136,8 +139,8 @@
         return jnp.where(plane == BX - 1, rim[:, slot + 1 : slot + 2], cells)
 
     even, odd = both[:PLANE], both[PLANE:]
-    rows = (low_row, edged(even + odd, 0), edged(even - odd, 2), high_row)
-    return [depth_back(cells, depth_out[h]) for cells in rows]
+    yield 1, depth_back(edged(even + odd, 0), depth_out[h])
+    yield 2, depth_back(edged(even - odd, 2), depth_out[h])
 
 
 def depth_back(cells, table):
@@ -159,6 +162,8 @@
         src,
         sent,
         got,
+        held_modes,
+        extras,
         base,
         inverse,
         toward_low,
@@ -205,13 +210,14 @@
 
         def column(far, carry):
             to_pz = wrapped(pz + far, PZ)
-            for near in range(PY):
+            for near in (4, 3, 5, 2, 6, 1, 7, 0):
                 one(near, to_pz)
             return carry
 
+        lax.fori_loop(PZ // 2, PZ, column, 0)
+        lax.fori_loop(1, PZ // 2, column, 0)
         for near in range(1, PY):
             one(near, pz)
-        lax.fori_loop(1, PZ, column, 0)
 
     barrier = pltpu.get_barrier_semaphore()
 
@@ -233,9 +239,9 @@
     ]
     early = fetches[:EARLY] + fetches[9:11]
     late = fetches[EARLY:9] + fetches[11:]
+    everyone(greet)
     for start in smalls + loads + early:
         start.start()
-    everyone(greet)
     for step in range(1, BLOCKS):
         pl.semaphore_signal(
             barrier, inc=1, device_id=(wrapped(blk + step, BLOCKS), py, pz), device_id_type=MESH
@@ -288,17 +294,17 @@
         part = slice(PLANE * h, PLANE * (h + 1))
         for r in range(2):
             for x in range(2):
-                sent[h, pl.ds(2 * r + x, PLANE, stride=SLOTS), :] = outer_cells[r][
+                sent[h, pl.ds(2 * r + x, PLANE, stride=THERE[h]), :] = outer_cells[r][
                     part, 128 * x : 128 * (x + 1)
                 ]
-        sent[h, pl.ds(4, PLANE, stride=SLOTS), :] = rim[part]
+    sent[0, pl.ds(4, PLANE, stride=THERE[0]), :] = rim[:PLANE] + pltpu.roll(rim[PLANE:], 4, 1)
 
     pl.semaphore_wait(barrier, PLANE - 1 + BLOCKS - 1)
 
-    def tile(d):
-        return pl.ds(d * SLOTS, SLOTS)
-
-    def exchange(src_ref, dst_ref, send_sem, recv_sem, h):
+    def exchange(src_ref, dst_ref, send_sem, recv_sem, h, slots):
+        def tile(d):
+            return pl.ds(d * slots, slots)
+
         def send(to_py, to_pz, to):
             pltpu.make_async_remote_copy(
                 src_ref=src_ref.at[h, tile(to), :],
@@ -312,8 +318,8 @@
         everyone(send)
         dst_ref[h, tile(place), :] = src_ref[h, tile(place), :]
 
-    def all_of(src_ref, dst_ref, send_sem, recv_sem, h):
-        others = pl.ds(0, (PLANE - 1) * SLOTS)
+    def all_of(src_ref, dst_ref, send_sem, recv_sem, h, slots):
+        others = pl.ds(0, (PLANE - 1) * slots)
         return pltpu.make_async_remote_copy(
             src_ref=src_ref.at[h, others, :],
             dst_ref=dst_ref.at[h, others, :],
@@ -324,7 +330,7 @@
         )
 
     for h in range(HALVES):
-        exchange(sent, got, go_send, go_recv, h)
+        exchange(sent, got, go_send, go_recv, h, THERE[h])
 
     for fetch in late:
         fetch.wait()
@@ -425,17 +431,20 @@
     change_2 = jnp.zeros((1, MODES), F32)
     total_squares = jnp.zeros((1, 1), F32)
     zero = jnp.zeros((1, MODES), F32)
-    for h in range(HALVES):
-        table, ratio = greens[h]
-        all_of(sent, got, go_send, go_recv, h).wait_recv()
-        plane = jnp.concatenate([outer_row(got, h, r) for r in range(2)], axis=0)
+    def leave_ends(h):
+        all_of(sent, got, go_send, go_recv, h, THERE[h]).wait_recv()
+        plane = jnp.concatenate([outer_row(got, h, r, THERE[h]) for r in range(2)], axis=0)
         held = times_right(plane.T, (outer_rows[0], outer_rows[1]), NN)
-        extra = times_right(row_of(got, h, 4).T, (inner_rows[0], inner_rows[1]), NN)
-        one, two = extra[:, :MODES], extra[:, MODES:]
-        at_first = one[0:1] + two[2:3]
-        at_last = one[127:128] + two[1:2]
-        cut_low = (one[OV : OV + 1] + two[OV + 2 : OV + 3]) * c0
-        cut_high = (one[OV - 1 : OV] + two[OV + 1 : OV + 2]) * c0
+        if h == 0:
+            extra = times_right(row_of(got, 0, 4, THERE[0]).T, (inner_rows[0], inner_rows[1]), NN)
+            for half in range(HALVES):
+                for i, lane_of in enumerate((0, 127, OV, OV - 1)):
+                    a, b = (lane_of + 4 * half) % 128, (lane_of + 4 * half + 2) % 128
+                    extras[half, i : i + 1, :] = extra[a : a + 1, :MODES] + extra[b : b + 1, MODES:]
+        at_first = extras[h, 0:1, :]
+        at_last = extras[h, 1:2, :]
+        cut_low = extras[h, 2:3, :] * c0
+        cut_high = extras[h, 3:4, :] * c0
         held = jnp.concatenate(
             [
                 held[:8] + jnp.where(row_id == 0, at_first, 0.0),
@@ -456,9 +465,14 @@
         for step in range(1, BLOCKS):
             to_ends(h, step).start()
 
-        solved_modes = times((planes_in[0], planes_in[1]), held, NN) * inverse[h]
+        held_modes[h] = held
+
+    def solve_own(h):
+        solved_modes = times((planes_in[0], planes_in[1]), held_modes[h], NN) * inverse[h]
         base[h] = times((planes_out[0], planes_out[1]), solved_modes, NN)
 
+    def give_back(h, total_squares, change_1, change_2):
+        table, ratio = greens[h]
         for step in range(1, BLOCKS):
             to_ends(h, step).wait_recv()
         tiles = [ends_in[h, b] for b in range(BLOCKS)]
@@ -534,11 +548,20 @@
         rim_modes = jnp.concatenate([rim_modes, jnp.zeros((120, 2 * MODES), F32)], axis=0)
         for r in range(2):
             for x in range(2):
-                back[h, pl.ds(2 * r + x, PLANE, stride=SLOTS), :] = plane[
+                back[h, pl.ds(2 * r + x, PLANE, stride=BACK), :] = plane[
                     PLANE * r : PLANE * (r + 1), 128 * x : 128 * (x + 1)
                 ]
-        back[h, pl.ds(4, PLANE, stride=SLOTS), :] = times((inner_rows[0], inner_rows[1]), rim_modes, NT)
-        exchange(back, returned, back_send, back_recv, h)
+        back[h, pl.ds(4, PLANE, stride=BACK), :] = times((inner_rows[0], inner_rows[1]), rim_modes, NT)
+        exchange(back, returned, back_send, back_recv, h, BACK)
+        return total_squares, change_1, change_2
+
+    sums = (total_squares, change_1, change_2)
+    leave_ends(0)
+    solve_own(0)
+    leave_ends(1)
+    sums = give_back(0, *sums)
+    solve_own(1)
+    give_back(1, *sums)
 
     for step in range(1, PZ):
         norm_copy(norm_out, norm_x, 0, step).wait_recv()
@@ -548,38 +571,37 @@
     for step in range(1, PY):
         norm_copy(norm_mid, norm_z, 1, step).start()
 
-    all_of(back, returned, back_send, back_recv, 0).wait_recv()
-    for r, cells in enumerate(
-        restored(returned, 0, local, by_row, by_plane, inner, inner_back, rims, depth_out)
-    ):
+    all_of(back, returned, back_send, back_recv, 0, BACK).wait_recv()
+    for r, cells in restored(returned, 0, local, by_row, by_plane, inner, inner_back, rims, depth_out):
         partial_out[r] = cells
 
     for h in range(HALVES):
-        all_of(sent, got, go_send, go_recv, h).wait_send()
+        all_of(sent, got, go_send, go_recv, h, THERE[h]).wait_send()
         for step in range(1, BLOCKS):
             to_ends(h, step).wait_send()
     for step in range(1, PZ):
         norm_copy(norm_out, norm_x, 0, step).wait_send()
-    all_of(back, returned, back_send, back_recv, 0).wait_send()
-    all_of(back, returned, back_send, back_recv, 1).wait_recv()
+    all_of(back, returned, back_send, back_recv, 0, BACK).wait_send()
+    all_of(back, returned, back_send, back_recv, 1, BACK).wait_recv()
     for step in range(1, PY):
         norm_copy(norm_mid, norm_z, 1, step).wait_recv()
-    all_of(back, returned, back_send, back_recv, 1).wait_send()
+    all_of(back, returned, back_send, back_recv, 1, BACK).wait_send()
     for step in range(1, PY):
         norm_copy(norm_mid, norm_z, 1, step).wait_send()
 
 
 def finish(returned, partial_out, norm_z, *refs):
-    held, (out, norms, result, out_sem) = refs[:-4], refs[-4:]
-    copies = []
-    for r, cells in enumerate(restored(returned, 1, *held)):
-        result[r] = partial_out[r] + cells
-        copies.append(pltpu.make_async_copy(result.at[r], out.at[r], out_sem.at[r]))
-        copies[r].start()
+    held, (out, norms, result, roots, out_sem, norm_sem) = refs[:-6], refs[-6:]
     lane = lax.broadcasted_iota(jnp.int32, (1, 128), 1)
     root = jnp.sqrt(sum(norm_z[i] for i in range(PY)) / CELLS)
     for i in range(3):
-        norms[i] = jnp.sum(jnp.where(lane == i, root, 0.0))
+        roots[i] = jnp.sum(jnp.where(lane == i, root, 0.0))
+    copies = [pltpu.make_async_copy(roots, norms, norm_sem)]
+    copies[0].start()
+    for r, cells in restored(returned, 1, *held):
+        result[r] = partial_out[r] + cells
+        copies.append(pltpu.make_async_copy(result.at[r], out.at[r], out_sem.at[r]))
+        copies[-1].start()
     for copy in copies:
         copy.wait()
 
@@ -587,10 +609,9 @@
 def shards(source, conduct, neighbours, orient):
     consts = tables()
     any_space = pl.BlockSpec(memory_space=pltpu.HBM)
-    smem = pl.BlockSpec(memory_space=pltpu.SMEM)
     vmem = pl.BlockSpec(memory_space=pltpu.VMEM)
     dma = pltpu.SemaphoreType.DMA
-    chunked = (HALVES, PLANE * SLOTS, 128)
+    chunked = (HALVES, PLANE * BACK, 128)
     modal = (HALVES, 2 * PLANE, BX)
     cells = pltpu.VMEM((ROWS, BX, NZ), F32)
     limit = 24 * 1024 * 1024
@@ -617,6 +638,8 @@
             cells,
             pltpu.VMEM(chunked, F32),
             pltpu.VMEM(chunked, F32),
+            pltpu.VMEM((HALVES, BX, MODES), F32),
+            pltpu.VMEM((HALVES, 8, MODES), F32),
             pltpu.VMEM((HALVES, BX, MODES), F32),
             pltpu.VMEM((HALVES, EXT, MODES), F32),
             pltpu.VMEM((HALVES, BX, MODES), F32),
@@ -663,8 +686,8 @@
             jax.ShapeDtypeStruct((3,), F32),
         ),
         in_specs=[vmem] * 10,
-        out_specs=(any_space, smem),
-        scratch_shapes=[cells, dma((ROWS,))],
+        out_specs=(any_space, any_space),
+        scratch_shapes=[cells, pltpu.SMEM((3,), F32), dma((ROWS,)), dma],
         compiler_params=pltpu.CompilerParams(vmem_limit_bytes=limit),
     )(*handed)
 

time: 40.1 us -> 37.3 us (0.930)
  Pallas kernels: 39.4 us -> 36.6 us
    pallas_call x1, Pallas kernels: 37.3 us -> 35 us  [shards(): pl.pallas_call(kernel, name='schwarz', out_shape=(jax.ShapeDtypeStruct(ch...]
    pallas_call x1, Pallas kernels: 2.03 us -> 1.62 us  [shards(): pl.pallas_call(finish, name='finish', out_shape=(jax.ShapeDtypeStruct((RO...]
where the time goes in v4:
time: 37.3 us; the launch traced here: 37.2 us
  Pallas kernels  36.6 us (98%)
  between operations  0.64 us (2%)
    pallas_call x1, Pallas kernels, shards(): pl.pallas_call(kernel, name='schwarz', out_shape=(jax.ShapeDtypeStruct(ch...  35 us
    pallas_call x1, Pallas kernels, shards(): pl.pallas_call(finish, name='finish', out_shape=(jax.ShapeDtypeStruct((RO...  1.62 us

profile of v4, /device:TPU:1, one launch (start us, length us, event | category | flops | bytes accessed | tf_op | source)
XLA Modules:
  0.0 37.2 jit_solution(15008297548088368781)
XLA Ops:
  0.6 35.0 %schwarz.1 = (f32[2,320,128]{2,1,0:T(8,128)S(1)}, f32[4,256,128]{2,1,0:T(8,128)S(1)}, f32[8,1,128]{2,1,0:T(1,128)S(1)}, f32[2,128,256]{2,1,0:T(8,128)S(1)}, f32[...) custom-call(f32[4,256,128]{2,1,0:T(8,128)} %source.1, ...), custom_call_target="tpu_custom_call" | custom-call | tf_op jit(solution)/shard_map/schwarz/pallas_call | solution.py:618
  35.6 1.6 %finish.1 = (f32[4,256,128]{2,1,0:T(8,128)}, f32[3]{0:T(128)}) custom-call(f32[2,320,128]{2,1,0:T(8,128)S(1)} %get-tuple-element.12.returned, f32[4,256,128]{2,1,0:T(8,128)S(1)} %get-tuple-element.13.partial_out, f32[8,1,128]{2,1,0:T(1,128)S(1)} %get-tuple-element.14.norm_z, f32[2,128,256]{2,1,0:T(8,128)S(1)} %get-tuple-element.15.refs_0_, ...), custom_call_target="tpu_custom_call" | custom-call | tf_op jit(solution)/shard_map/finish/pallas_call | solution.py:681

commit v5 on v4

--- a/solution.py
+++ b/solution.py
@@ -198,26 +198,25 @@
     def wrapped(a, n):
         return jnp.where(a >= n, a - n, a)
 
-    def peer(step):
-        to_py = wrapped(py + step % PY, PY)
-        to_pz = wrapped(pz + step // PY, PZ)
-        return to_py, to_pz, to_py * PZ + to_pz
-
-    def everyone(visit):
+    core = lax.rem(pz, 2)
+    chip = pz // 2
+
+    def everyone(visit, first_core):
         def one(near, to_pz):
             to_py = wrapped(py + near, PY)
             visit(to_py, to_pz, to_py * PZ + to_pz)
 
-        def column(far, carry):
-            to_pz = wrapped(pz + far, PZ)
-            for near in (4, 3, 5, 2, 6, 1, 7, 0):
-                one(near, to_pz)
+        def group(turn, carry):
+            to_core = turn if first_core == 0 else 1 - turn
+            for far in (2, 1, 3):
+                for near in (4, 3, 5, 2, 6, 1, 7, 0):
+                    one(near, wrapped(chip + far, PZ // 2) * 2 + to_core)
+            for near in (4, 3, 5, 2, 6, 1, 7):
+                one(near, chip * 2 + to_core)
             return carry
 
-        lax.fori_loop(PZ // 2, PZ, column, 0)
-        lax.fori_loop(1, PZ // 2, column, 0)
-        for near in range(1, PY):
-            one(near, pz)
+        one(0, chip * 2 + 1 - core)
+        lax.fori_loop(0, 2, group, 0)
 
     barrier = pltpu.get_barrier_semaphore()
 
@@ -239,7 +238,7 @@
     ]
     early = fetches[:EARLY] + fetches[9:11]
     late = fetches[EARLY:9] + fetches[11:]
-    everyone(greet)
+    everyone(greet, 0)
     for start in smalls + loads + early:
         start.start()
     for step in range(1, BLOCKS):
@@ -301,7 +300,7 @@
 
     pl.semaphore_wait(barrier, PLANE - 1 + BLOCKS - 1)
 
-    def exchange(src_ref, dst_ref, send_sem, recv_sem, h, slots):
+    def exchange(src_ref, dst_ref, send_sem, recv_sem, h, slots, first_core):
         def tile(d):
             return pl.ds(d * slots, slots)
 
@@ -315,7 +314,7 @@
                 device_id_type=MESH,
             ).start()
 
-        everyone(send)
+        everyone(send, first_core)
         dst_ref[h, tile(place), :] = src_ref[h, tile(place), :]
 
     def all_of(src_ref, dst_ref, send_sem, recv_sem, h, slots):
@@ -330,7 +329,7 @@
         )
 
     for h in range(HALVES):
-        exchange(sent, got, go_send, go_recv, h, THERE[h])
+        exchange(sent, got, go_send, go_recv, h, THERE[h], 0)
 
     for fetch in late:
         fetch.wait()
@@ -552,7 +551,7 @@
                     PLANE * r : PLANE * (r + 1), 128 * x : 128 * (x + 1)
                 ]
         back[h, pl.ds(4, PLANE, stride=BACK), :] = times((inner_rows[0], inner_rows[1]), rim_modes, NT)
-        exchange(back, returned, back_send, back_recv, h, BACK)
+        exchange(back, returned, back_send, back_recv, h, BACK, 1)
         return total_squares, change_1, change_2
 
     sums = (total_squares, change_1, change_2)

time: 37.3 us -> 37.1 us (level)
  no operation moved by 1% of the time
where the time goes in v5:
time: 37.1 us; the launch traced here: 37 us
  Pallas kernels  36.4 us (98%)
  between operations  0.64 us (2%)
    pallas_call x1, Pallas kernels, shards(): pl.pallas_call(kernel, name='schwarz', out_shape=(jax.ShapeDtypeStruct(ch...  34.8 us
    pallas_call x1, Pallas kernels, shards(): pl.pallas_call(finish, name='finish', out_shape=(jax.ShapeDtypeStruct((RO...  1.61 us

profile of v5, /device:TPU:1, one launch (start us, length us, event | category | flops | bytes accessed | tf_op | source)
XLA Modules:
  0.0 37.0 jit_solution(1129154921280897821)
XLA Ops:
  0.6 34.8 %schwarz.1 = (f32[2,320,128]{2,1,0:T(8,128)S(1)}, f32[4,256,128]{2,1,0:T(8,128)S(1)}, f32[8,1,128]{2,1,0:T(1,128)S(1)}, f32[2,128,256]{2,1,0:T(8,128)S(1)}, f32[...) custom-call(f32[4,256,128]{2,1,0:T(8,128)} %source.1, ...), custom_call_target="tpu_custom_call" | custom-call | tf_op jit(solution)/shard_map/schwarz/pallas_call | solution.py:617
  35.4 1.6 %finish.1 = (f32[4,256,128]{2,1,0:T(8,128)}, f32[3]{0:T(128)}) custom-call(f32[2,320,128]{2,1,0:T(8,128)S(1)} %get-tuple-element.12.returned, f32[4,256,128]{2,1,0:T(8,128)S(1)} %get-tuple-element.13.partial_out, f32[8,1,128]{2,1,0:T(1,128)S(1)} %get-tuple-element.14.norm_z, f32[2,128,256]{2,1,0:T(8,128)S(1)} %get-tuple-element.15.refs_0_, ...), custom_call_target="tpu_custom_call" | custom-call | tf_op jit(solution)/shard_map/finish/pallas_call | solution.py:680

commit v6 on v5

--- a/solution.py
+++ b/solution.py
@@ -28,7 +28,7 @@
 NT = (((1,), (1,)), ((), ()))
 CELLS = float(BLOCKS * BX * NY * NZ)
 TN = (((0,), (0,)), ((), ()))
-BACK = 5
+BACK = (4, 5)
 THERE = (5, 4)
 CONSTS = 13
 EARLY = 3
@@ -62,10 +62,12 @@
     inner = np.zeros((BX, BX))
     inner[1:-1, :-2] = basis(BX - 2)
     mu_inner = np.concatenate([eigenvalues(BX - 2), np.ones(2)])[None, :]
-    rims = np.zeros((128, 2 * BX))
-    rims[:4] = np.concatenate(
-        [np.stack([inner[1], inner[-2]] * 2), np.stack([inner[1], inner[-2], -inner[1], -inner[-2]])], axis=1
-    )
+    rims = np.zeros((8, HALVES * 2 * BX))
+    for h in range(HALVES):
+        columns = slice(2 * BX * h, 2 * BX * (h + 1))
+        rims[4 * h : 4 * h + 4, columns] = np.concatenate(
+            [np.stack([inner[1], inner[-2]] * 2), np.stack([inner[1], inner[-2], -inner[1], -inner[-2]])], axis=1
+        )
     planes_in = planes[OV : OV + BX].T
     depth_in = np.concatenate([depth[0], depth[0], depth[1]], axis=1)
     depth_out = np.stack(
@@ -118,29 +120,15 @@
     return jnp.concatenate([row_of(ref, h, 2 * r + x, slots) for x in range(2)], axis=1)
 
 
-def restored(returned, h, local, by_row, by_plane, inner, inner_back, rims, depth_out):
-    low_row = outer_row(returned, h, 0, BACK)
-    high_row = outer_row(returned, h, 1, BACK)
-    yield 0, depth_back(low_row, depth_out[h])
-    yield 3, depth_back(high_row, depth_out[h])
-    rim = row_of(returned, h, 4, BACK)
-    from_rows = times_right(
-        jnp.concatenate([low_row + high_row, low_row - high_row], axis=0), (inner[0], inner[1]), NN
-    )
-    from_rim = times_right(rim, (rims[0], rims[1]), NN)
-    from_rim = jnp.concatenate([from_rim[:, :BX], from_rim[:, BX:]], axis=0)
-    both = times_right(
-        local[h] + by_row[h] * from_rows + by_plane[h] * from_rim, (inner_back[0], inner_back[1]), NN
-    )
-    plane = lax.broadcasted_iota(jnp.int32, (PLANE, BX), 1)
-
-    def edged(cells, slot):
-        cells = jnp.where(plane == 0, rim[:, slot : slot + 1], cells)
-        return jnp.where(plane == BX - 1, rim[:, slot + 1 : slot + 2], cells)
-
-    even, odd = both[:PLANE], both[PLANE:]
-    yield 1, depth_back(edged(even + odd, 0), depth_out[h])
-    yield 2, depth_back(edged(even - odd, 2), depth_out[h])
+def outer_restored(returned, h, depth_out):
+    low_row = outer_row(returned, h, 0, BACK[h])
+    high_row = outer_row(returned, h, 1, BACK[h])
+    mixed = jnp.concatenate([low_row + high_row, low_row - high_row], axis=0)
+    return depth_back(low_row, depth_out[h]), depth_back(high_row, depth_out[h]), mixed
+
+
+def rows_of(both):
+    return both[:PLANE] + both[PLANE:], both[:PLANE] - both[PLANE:]
 
 
 def depth_back(cells, table):
@@ -164,6 +152,7 @@
         got,
         held_modes,
         extras,
+        rim_held,
         base,
         inverse,
         toward_low,
@@ -537,21 +526,24 @@
         across = base[h] + toward_low[h] * at_low + toward_high[h] * at_high
         plane = times((outer_rows[0], outer_rows[1]), across, NT)
         ends = [across[:1], across[-1:]]
-        rim_modes = jnp.concatenate(
+        edge_modes = jnp.concatenate(
             [
-                sum(jnp.where(row_id == 2 * r + e, ends[e], 0.0) for e in range(2))
+                sum(jnp.where(row_id == 4 * h + 2 * r + e, ends[e], 0.0) for e in range(2))
                 for r in range(2)
             ],
             axis=1,
         )
-        rim_modes = jnp.concatenate([rim_modes, jnp.zeros((120, 2 * MODES), F32)], axis=0)
         for r in range(2):
             for x in range(2):
-                back[h, pl.ds(2 * r + x, PLANE, stride=BACK), :] = plane[
+                back[h, pl.ds(2 * r + x, PLANE, stride=BACK[h]), :] = plane[
                     PLANE * r : PLANE * (r + 1), 128 * x : 128 * (x + 1)
                 ]
-        back[h, pl.ds(4, PLANE, stride=BACK), :] = times((inner_rows[0], inner_rows[1]), rim_modes, NT)
-        exchange(back, returned, back_send, back_recv, h, BACK, 1)
+        if h == 0:
+            rim_held[...] = edge_modes
+        else:
+            rim_modes = jnp.concatenate([rim_held[...] + edge_modes, jnp.zeros((120, 2 * MODES), F32)], axis=0)
+            back[h, pl.ds(4, PLANE, stride=BACK[h]), :] = times((inner_rows[0], inner_rows[1]), rim_modes, NT)
+        exchange(back, returned, back_send, back_recv, h, BACK[h], 1)
         return total_squares, change_1, change_2
 
     sums = (total_squares, change_1, change_2)
@@ -570,9 +562,12 @@
     for step in range(1, PY):
         norm_copy(norm_mid, norm_z, 1, step).start()
 
-    all_of(back, returned, back_send, back_recv, 0, BACK).wait_recv()
-    for r, cells in restored(returned, 0, local, by_row, by_plane, inner, inner_back, rims, depth_out):
-        partial_out[r] = cells
+    all_of(back, returned, back_send, back_recv, 0, BACK[0]).wait_recv()
+    partial_out[0], partial_out[3], mixed = outer_restored(returned, 0, depth_out)
+    from_rows = times_right(mixed, (inner[0], inner[1]), NN)
+    both = times_right(local[0] + by_row[0] * from_rows, (inner_back[0], inner_back[1]), NN)
+    for r, cells in enumerate(rows_of(both)):
+        partial_out[1 + r] = depth_back(cells, depth_out[0])
 
     for h in range(HALVES):
         all_of(sent, got, go_send, go_recv, h, THERE[h]).wait_send()
@@ -580,11 +575,11 @@
             to_ends(h, step).wait_send()
     for step in range(1, PZ):
         norm_copy(norm_out, norm_x, 0, step).wait_send()
-    all_of(back, returned, back_send, back_recv, 0, BACK).wait_send()
-    all_of(back, returned, back_send, back_recv, 1, BACK).wait_recv()
+    all_of(back, returned, back_send, back_recv, 0, BACK[0]).wait_send()
+    all_of(back, returned, back_send, back_recv, 1, BACK[1]).wait_recv()
     for step in range(1, PY):
         norm_copy(norm_mid, norm_z, 1, step).wait_recv()
-    all_of(back, returned, back_send, back_recv, 1, BACK).wait_send()
+    all_of(back, returned, back_send, back_recv, 1, BACK[1]).wait_send()
     for step in range(1, PY):
         norm_copy(norm_mid, norm_z, 1, step).wait_send()
 
@@ -597,10 +592,36 @@
         roots[i] = jnp.sum(jnp.where(lane == i, root, 0.0))
     copies = [pltpu.make_async_copy(roots, norms, norm_sem)]
     copies[0].start()
-    for r, cells in restored(returned, 1, *held):
+
+    def put(r, cells):
         result[r] = partial_out[r] + cells
         copies.append(pltpu.make_async_copy(result.at[r], out.at[r], out_sem.at[r]))
         copies[-1].start()
+
+    local, by_row, by_plane, inner, inner_back, rims, depth_out = held
+    low_cells, high_cells, mixed = outer_restored(returned, 1, depth_out)
+    put(0, low_cells)
+    put(3, high_cells)
+    rim = row_of(returned, 1, 4, BACK[1])[:, :8]
+    from_rim = times_right(rim, (rims[0], rims[1]), NN)
+    parts = [from_rim[:, BX * q : BX * (q + 1)] for q in range(4)]
+    from_rim = [jnp.concatenate(parts[2 * h : 2 * h + 2], axis=0) for h in range(HALVES)]
+    from_rows = times_right(mixed, (inner[0], inner[1]), NN)
+    second = local[1] + by_row[1] * from_rows + by_plane[1] * from_rim[1]
+    both = times_right(
+        jnp.concatenate([by_plane[0] * from_rim[0], second], axis=0), (inner_back[0], inner_back[1]), NN
+    )
+    plane = lax.broadcasted_iota(jnp.int32, (PLANE, BX), 1)
+    halves_of = [rows_of(both[2 * PLANE * h : 2 * PLANE * (h + 1)]) for h in range(HALVES)]
+    for r in range(2):
+        total = None
+        for h in range(HALVES):
+            slot = 4 * h + 2 * r
+            cells = jnp.where(plane == 0, rim[:, slot : slot + 1], halves_of[h][r])
+            cells = jnp.where(plane == BX - 1, rim[:, slot + 1 : slot + 2], cells)
+            cells = depth_back(cells, depth_out[h])
+            total = cells if total is None else total + cells
+        put(1 + r, total)
     for copy in copies:
         copy.wait()
 
@@ -610,7 +631,7 @@
     any_space = pl.BlockSpec(memory_space=pltpu.HBM)
     vmem = pl.BlockSpec(memory_space=pltpu.VMEM)
     dma = pltpu.SemaphoreType.DMA
-    chunked = (HALVES, PLANE * BACK, 128)
+    chunked = (HALVES, PLANE * max(BACK), 128)
     modal = (HALVES, 2 * PLANE, BX)
     cells = pltpu.VMEM((ROWS, BX, NZ), F32)
     limit = 24 * 1024 * 1024
@@ -639,6 +660,7 @@
             pltpu.VMEM(chunked, F32),
             pltpu.VMEM((HALVES, BX, MODES), F32),
             pltpu.VMEM((HALVES, 8, MODES), F32),
+            pltpu.VMEM((8, 2 * MODES), F32),
             pltpu.VMEM((HALVES, BX, MODES), F32),
             pltpu.VMEM((HALVES, EXT, MODES), F32),
             pltpu.VMEM((HALVES, BX, MODES), F32),

time: 37.1 us -> 36.6 us (0.987)
  Pallas kernels: 36.4 us -> 35.8 us
    pallas_call x1, Pallas kernels: 34.8 us -> 33.9 us  [shards(): pl.pallas_call(kernel, name='schwarz', out_shape=(jax.ShapeDtypeStruct(ch...]
where the time goes in v6:
time: 36.6 us; the launch traced here: 36.5 us
  Pallas kernels  35.8 us (98%)
  between operations  0.64 us (2%)
    pallas_call x1, Pallas kernels, shards(): pl.pallas_call(kernel, name='schwarz', out_shape=(jax.ShapeDtypeStruct(ch...  33.9 us
    pallas_call x1, Pallas kernels, shards(): pl.pallas_call(finish, name='finish', out_shape=(jax.ShapeDtypeStruct((RO...  1.92 us

profile of v6, /device:TPU:1, one launch (start us, length us, event | category | flops | bytes accessed | tf_op | source)
XLA Modules:
  0.0 36.5 jit_solution(11828249960442968398)
XLA Ops:
  0.6 33.9 %schwarz.1 = (f32[2,320,128]{2,1,0:T(8,128)S(1)}, f32[4,256,128]{2,1,0:T(8,128)S(1)}, f32[8,1,128]{2,1,0:T(1,128)S(1)}, f32[2,128,256]{2,1,0:T(8,128)S(1)}, f32[...) custom-call(f32[4,256,128]{2,1,0:T(8,128)} %source.1, ...), custom_call_target="tpu_custom_call" | custom-call | tf_op jit(solution)/shard_map/schwarz/pallas_call | solution.py:638
  34.5 1.9 %finish.1 = (f32[4,256,128]{2,1,0:T(8,128)}, f32[3]{0:T(128)}) custom-call(f32[2,320,128]{2,1,0:T(8,128)S(1)} %get-tuple-element.12.returned, f32[4,256,128]{2,1,0:T(8,128)S(1)} %get-tuple-element.13.partial_out, f32[8,1,128]{2,1,0:T(1,128)S(1)} %get-tuple-element.14.norm_z, f32[2,128,256]{2,1,0:T(8,128)S(1)} %get-tuple-element.15.refs_0_, ...), custom_call_target="tpu_custom_call" | custom-call | tf_op jit(solution)/shard_map/finish/pallas_call | solution.py:702

commit v7 on v6

--- a/solution.py
+++ b/solution.py
@@ -512,6 +512,26 @@
         at_high = sum(own_at[m] * (final[m][3] + ratio * final[m][2]) for m in range(BLOCKS))
         at_low, at_high = pick(own_flip, at_high, at_low), pick(own_flip, at_low, at_high)
 
+        across = base[h] + toward_low[h] * at_low + toward_high[h] * at_high
+        plane = times((outer_rows[0], outer_rows[1]), across, NT)
+        ends = [across[:1], across[-1:]]
+        edge_modes = jnp.concatenate(
+            [
+                sum(jnp.where(row_id == 4 * h + 2 * r + e, ends[e], 0.0) for e in range(2))
+                for r in range(2)
+            ],
+            axis=1,
+        )
+        for r in range(2):
+            for x in range(2):
+                back[h, pl.ds(2 * r + x, PLANE, stride=BACK[h]), :] = plane[
+                    PLANE * r : PLANE * (r + 1), 128 * x : 128 * (x + 1)
+                ]
+        if h == 0:
+            rim_held[...] = edge_modes
+        else:
+            rim_modes = jnp.concatenate([rim_held[...] + edge_modes, jnp.zeros((120, 2 * MODES), F32)], axis=0)
+            back[h, pl.ds(4, PLANE, stride=BACK[h]), :] = times((inner_rows[0], inner_rows[1]), rim_modes, NT)
         if h == HALVES - 1:
             partial = (
                 jnp.where(lane == 0, total_squares, 0.0)
@@ -523,26 +543,6 @@
             for step in range(1, PZ):
                 norm_copy(norm_out, norm_x, 0, step).start()
 
-        across = base[h] + toward_low[h] * at_low + toward_high[h] * at_high
-        plane = times((outer_rows[0], outer_rows[1]), across, NT)
-        ends = [across[:1], across[-1:]]
-        edge_modes = jnp.concatenate(
-            [
-                sum(jnp.where(row_id == 4 * h + 2 * r + e, ends[e], 0.0) for e in range(2))
-                for r in range(2)
-            ],
-            axis=1,
-        )
-        for r in range(2):
-            for x in range(2):
-                back[h, pl.ds(2 * r + x, PLANE, stride=BACK[h]), :] = plane[
-                    PLANE * r : PLANE * (r + 1), 128 * x : 128 * (x + 1)
-                ]
-        if h == 0:
-            rim_held[...] = edge_modes
-        else:
-            rim_modes = jnp.concatenate([rim_held[...] + edge_modes, jnp.zeros((120, 2 * MODES), F32)], axis=0)
-            back[h, pl.ds(4, PLANE, stride=BACK[h]), :] = times((inner_rows[0], inner_rows[1]), rim_modes, NT)
         exchange(back, returned, back_send, back_recv, h, BACK[h], 1)
         return total_squares, change_1, change_2
 

time: 36.6 us -> 36.9 us (level)
  Pallas kernels: 35.8 us -> 36.2 us
where the time goes in v7:
time: 36.9 us; the launch traced here: 36.8 us
  Pallas kernels  36.2 us (98%)
  between operations  0.64 us (2%)
    pallas_call x1, Pallas kernels, shards(): pl.pallas_call(kernel, name='schwarz', out_shape=(jax.ShapeDtypeStruct(ch...  34.3 us
    pallas_call x1, Pallas kernels, shards(): pl.pallas_call(finish, name='finish', out_shape=(jax.ShapeDtypeStruct((RO...  1.92 us

profile of v7, /device:TPU:1, one launch (start us, length us, event | category | flops | bytes accessed | tf_op | source)
XLA Modules:
  0.0 36.8 jit_solution(13134317765562035347)
XLA Ops:
  0.6 34.3 %schwarz.1 = (f32[2,320,128]{2,1,0:T(8,128)S(1)}, f32[4,256,128]{2,1,0:T(8,128)S(1)}, f32[8,1,128]{2,1,0:T(1,128)S(1)}, f32[2,128,256]{2,1,0:T(8,128)S(1)}, f32[...) custom-call(f32[4,256,128]{2,1,0:T(8,128)} %source.1, ...), custom_call_target="tpu_custom_call" | custom-call | tf_op jit(solution)/shard_map/schwarz/pallas_call | solution.py:638
  34.9 1.9 %finish.1 = (f32[4,256,128]{2,1,0:T(8,128)}, f32[3]{0:T(128)}) custom-call(f32[2,320,128]{2,1,0:T(8,128)S(1)} %get-tuple-element.12.returned, f32[4,256,128]{2,1,0:T(8,128)S(1)} %get-tuple-element.13.partial_out, f32[8,1,128]{2,1,0:T(1,128)S(1)} %get-tuple-element.14.norm_z, f32[2,128,256]{2,1,0:T(8,128)S(1)} %get-tuple-element.15.refs_0_, ...), custom_call_target="tpu_custom_call" | custom-call | tf_op jit(solution)/shard_map/finish/pallas_call | solution.py:702
